TPU v7x, 256 devices: a whole 4x4x8 slice. The times are simulated.
256 devices in a mesh: grp: 4 (over y), dev: 64 (over x, z, core).
Axes of the slice: x: 4, y: 4, z: 8, core: 2. Of those that a mesh axis runs over, the one named last changes fastest.
Arguments:
- pool_rows: bfloat16 [262144, 1024], P(('grp', 'dev')), may hold values from -6 to 6
- sample_index: int32 [262144], P(('grp', 'dev')), may hold values from 0 to 262143, as said below
- cluster_id: int32 [262144], P(('grp', 'dev')), may hold values from 0 to 511, as said below
- child_id: int32 [262144], P(('grp', 'dev')), may hold values from 0 to 7
- old_centroids: float32 [512, 8, 1024], P('dev'), may hold values from -6 to 6
Outputs:
- centroids: float32 [512, 8, 1024], P('dev')
- child_counts: int32 [512, 8], P('dev')
Inputs may be any that keep to these rules, and one draw needn't show every extreme that they name: Sample i takes a pool row of its own aligned block of 1024 rows: sample_index[i] // 1024 == i // 1024. `cluster_id`: in each aligned block of 1024 samples (the rows of one device) the 2 clusters o * 2 to o * 2 + 1 of any owner o are named at most 8 times together, and one cluster, the same in every block, is named exactly 8 times in every block.
All inputs are finite; a program needn't handle non-finite values.
Results may differ from a plain program's by a relative error of at most 0.0003.
Values may be sent and summed in bfloat16 or wider, within the bound.
No kernel may reach another device: no remote copies, remote signals or barrier semaphores. Data moves between devices by JAX's collectives and lax.ppermute only.
A program may use at most 64 MiB of HBM per device.

v0:
```python
import functools

import jax
import jax.numpy as jnp
from jax import lax
from jax.experimental import pallas as pl
from jax.experimental.pallas import tpu as pltpu
from jax.sharding import Mesh, PartitionSpec as P


AXES = ("y", "x", "zh", "zl", "c")
SIZES = (4, 4, 4, 2, 2)
N, ZH, ZL, NC = 4, 4, 2, 2
NZ = ZH * ZL
CHUNKS = N * ZL
LANES = 128
TILE = 8
LOW = 32
VMEM = pltpu.VMEM
SMEM = pltpu.SMEM
HBM = pltpu.HBM
DMA = pltpu.SemaphoreType.DMA

RAW = [(2, 1), (2, 0), (0, 1), (1, 1), (3, 0), (3, 1), (1, 0)]
FIRST = 3
DEEP = [0, 2, 1, 3]
TURNS = [0, 1, 3, 2]
EARLY = 4


def permute(value, move):
    pairs = []
    for y in range(N):
        for x in range(N):
            for z in range(NZ):
                for c in range(NC):
                    ty, tx, tz, tc = move(y, x, z, c)
                    to = (((ty % N) * N + tx % N) * NZ + tz % NZ) * NC + tc % NC
                    pairs.append((((y * N + x) * NZ + z) * NC + c, to))
    return lax.ppermute(value, AXES, pairs)


def raw_move(step, swap):
    def move(y, x, z, c):
        if swap:
            z = z ^ 1 if c == 0 else (z + 1 if z % 2 else z - 1)
        return (y, x + step, z, c) if c == 0 else (y + step, x, z, c)

    return move


def cross_move(step):
    return lambda y, x, z, c: (y + step, x, z, c) if c == 0 else (y, x + step, z, c)


def iota(shape, dim):
    return lax.broadcasted_iota(jnp.int32, shape, dim)


def one_hot(mask, dtype=jnp.bfloat16):
    return jnp.where(mask, 1.0, 0.0).astype(dtype)


def dot(a, b, dims=((1,), (0,))):
    return lax.dot_general(a, b, (dims, ((), ())), preferred_element_type=jnp.float32)


def shape(*dims, dtype=jnp.float32):
    return jax.ShapeDtypeStruct(dims, dtype)


def call(kernel, outs, spaces, args, scratch=()):
    return pl.pallas_call(
        kernel,
        out_shape=outs,
        in_specs=[pl.BlockSpec(memory_space=s) for s in spaces],
        out_specs=jax.tree.map(lambda _: pl.BlockSpec(memory_space=VMEM), outs),
        scratch_shapes=list(scratch),
        compiler_params=pltpu.CompilerParams(vmem_limit_bytes=44 << 20),
    )(*args)


def ranks(hot, mask):
    owners, rows = hot.shape
    wide = (LANES, 2 * LANES)
    before = one_hot((iota(wide, 0) < iota(wide, 1)) | (iota(wide, 1) >= LANES))
    seen = jnp.zeros((owners, LANES), jnp.float32)
    out = []
    for b in range(rows // LANES):
        at = slice(b * LANES, (b + 1) * LANES)
        counted = dot(hot[:, at], before)
        out.append(jnp.sum(jnp.where(mask[:, at], counted[:, :LANES] + seen, 0.0), axis=0, keepdims=True))
        seen = seen + counted[:, LANES:]
    return jnp.concatenate(out, axis=1).astype(jnp.int32)


def lines_of(where, most, owned, kinds, ints):
    a_me, b_me, odd, z_me, core = where[0], where[1], where[2], where[3], where[4]
    rows = ints.shape[2]
    index, cluster, child = ints[0], ints[1], ints[2]
    owner = lax.div(cluster, owned)
    quarter = lax.rem(owner, N)
    dev = lax.div(owner, N)
    to_core = lax.rem(dev, NC)
    z = lax.rem(lax.div(dev, NC), NZ)
    x = lax.div(dev, NC * NZ)
    a = x + (quarter - x) * core
    b = quarter + (x - quarter) * core
    step = lax.rem(a - a_me + N, N)
    swap = lax.rem(lax.rem(z, ZL) + odd, ZL)
    b = lax.rem(b - b_me + N, N)
    pair = lax.rem(lax.div(z, ZL) - z_me + swap * core * (1 - 2 * odd) + 2 * ZH, ZH)
    spot = ((step * ZL + swap) * N + b) * (ZH * NC) + pair * NC + lax.rem(to_core + core, NC)
    spots = N * N * NZ * NC
    mask = iota((spots, rows), 0) == spot
    hot = one_hot(mask)
    rank = iota((most, rows), 0) == ranks(hot, mask)
    index = lax.rem(index, rows) + 1
    label = lax.rem(cluster, owned) * kinds + child + 1

    high = lax.div(index, LOW)
    lines = [jnp.where(rank, a.astype(jnp.float32), 0.0) for a in (index - high * LOW, high * LOW, label)]
    spread = dot(hot, jnp.concatenate(lines, axis=0).astype(jnp.bfloat16), ((1,), (1,)))
    source = spread[:, :most] + spread[:, most : 2 * most]
    per = LANES // most
    tile = one_hot(iota((most, LANES), 0) == lax.rem(iota((most, LANES), 1), most))
    label = dot(spread[:, 2 * most :].astype(jnp.bfloat16), tile)
    keep = lax.div(iota((spots, LANES), 1), most) == lax.rem(iota((spots, LANES), 0), per)
    label = jnp.sum(jnp.where(keep, label, 0.0).reshape(spots // per, per, LANES), axis=1)
    return source, label


def lines_kernel(most, owned, kinds, where, ints_ref, source_ref, label_ref):
    source_ref[...], label_ref[...] = lines_of(where, most, owned, kinds, ints_ref)


def pool_kernel(most, owned, kinds, where, ints_ref, pool_hbm, source_ref, label_ref, pool, sem):
    width = pool.shape[1]
    columns = pl.ds(pl.multiple_of(where[4] * width, width), width)
    copy = pltpu.make_async_copy(pool_hbm.at[:, columns], pool, sem)
    copy.start()
    source_ref[...], label_ref[...] = lines_of(where, most, owned, kinds, ints_ref)
    copy.wait()


def fill_kernel(chunks, where, own_source, own_label, came_source, came_label, own_pool, came_pool, *rest):
    outs, select = rest[:-1], rest[-1]
    rows, width = own_pool.shape
    blocks = width // LANES
    most = own_source.shape[1]
    spots = own_source.shape[0] // CHUNKS
    chunk = spots * most
    pick = iota((chunk, most), 1) == lax.rem(iota((chunk, most), 0), most)
    lines = chunk // LANES
    line = iota((TILE, LANES), 0)
    for i, j in enumerate(chunks):
        tile = jnp.zeros((TILE, LANES), jnp.float32)
        for k, (source_ref, label_ref) in enumerate(((own_source, own_label), (came_source, came_label))):
            source = source_ref[j * spots : (j + 1) * spots, :]
            source = jnp.broadcast_to(source[:, None, :], (spots, most, most)).reshape(chunk, most)
            source = jnp.sum(jnp.where(pick, source, 0.0), axis=1, keepdims=True).astype(jnp.int32)
            select[k, i * chunk : (i + 1) * chunk, :] = one_hot(iota((chunk, rows), 1) + 1 == source)
            for h in range(lines):
                tile = jnp.where(line == k * lines + h, label_ref[j * lines + h : j * lines + h + 1, :], tile)
        outs[i][blocks * NC * chunk :, :] = tile.astype(jnp.bfloat16)
    columns = pl.ds(pl.multiple_of(where[4] * width, width), width)
    for k in range(NC):
        pool = came_pool[:, columns] if k else own_pool[...]
        for g in range(0, len(chunks), 2):
            some = min(2, len(chunks) - g)
            got = dot(select[k, g * chunk : (g + some) * chunk, :], pool).astype(jnp.bfloat16)
            for i in range(some):
                for b in range(blocks):
                    at = (b * NC + k) * chunk
                    outs[g + i][at : at + chunk, :] = got[i * chunk : (i + 1) * chunk, b * LANES : (b + 1) * LANES]


def add_up(most, kinds2, ins, h, before=None):
    chunk = N * ZH * NC * most
    blocks = (ins[0].shape[0] - TILE) // (NC * chunk)
    lines = chunk // LANES
    segments = LANES // most * kinds2
    row = iota((segments, LANES), 0)
    base = lax.div(iota((1, LANES), 1), most) * kinds2 - 1
    ones = jnp.ones((TILE, 2 * NC * LANES), jnp.bfloat16)
    sums, count = before if before is not None else (0.0, 0.0)
    for j in range(0, len(ins), 2):
        hots, data = [], []
        for r in ins[j : j + 2]:
            labels = r[blocks * NC * chunk :, :].astype(jnp.float32).astype(jnp.int32)
            for k in range(NC):
                label = labels[k * lines + h : k * lines + h + 1]
                hots.append(one_hot(row == jnp.where(label > 0, base + label, -1)))
                first = [(b * NC + k) * chunk + h * LANES for b in range(blocks)]
                data.append(jnp.concatenate([r[i : i + LANES, :] for i in first], axis=1))
        hot = jnp.concatenate(hots, axis=1)
        sums = sums + dot(hot, jnp.concatenate(data, axis=0))
        count = count + dot(ones, hot, ((1,), (1,)))
    return sums, count


def early_kernel(most, kinds2, *rest):
    ins, (total, tally) = rest[:-2], rest[-2:]
    lines = tally.shape[0]
    segments = total.shape[0] // lines
    for h in range(lines):
        total[h * segments : (h + 1) * segments, :], tally[h] = add_up(most, kinds2, ins, h)


def late_kernel(most, kinds2, sum_ref, tally_ref, *rest):
    ins, outs = rest[:-N], rest[-N:]
    lines = tally_ref.shape[0]
    segments = sum_ref.shape[0] // lines
    blocks = sum_ref.shape[1] // LANES
    part = lines * segments // N
    for h in range(lines):
        before = (sum_ref[h * segments : (h + 1) * segments, :], tally_ref[h])
        sums, count = add_up(most, kinds2, ins, h, before)
        for p in range(segments // part):
            out = outs[TURNS.index(h * (segments // part) + p)]
            for k in range(blocks):
                out[k * part : (k + 1) * part, :] = sums[p * part : (p + 1) * part, k * LANES : (k + 1) * LANES]
            out[blocks * part :, :] = count[:, p * part : (p + 1) * part]


def cross_kernel(*rest):
    ins, outs = rest[:N], rest[N:]
    part = outs[0].shape[0] - TILE
    blocks = (ins[0].shape[0] - TILE) // LANES
    some = part // blocks
    total = (ins[0][...] + ins[1][...]) + (ins[2][...] + ins[3][...])
    for step, out in zip(DEEP, outs):
        for k in range(blocks):
            out[k * some : (k + 1) * some, :] = total[k * LANES + step * some : k * LANES + (step + 1) * some]
        tile = total[blocks * LANES :]
        out[part:, :] = jnp.concatenate([tile[:, step * some :], tile[:, : step * some]], axis=1) if step else tile


def depth_kernel(some, *rest):
    ins, (other_ref, mine_ref) = rest[:ZH], rest[ZH:]
    total = (ins[0][...] + ins[1][...]) + (ins[2][...] + ins[3][...])
    part = other_ref.shape[0]
    for side, out in enumerate((mine_ref, other_ref)):
        for k in range(part // some):
            at = (k * NC + side) * some
            out[k * some : (k + 1) * some, :] = total[at : at + some]
    mine_ref[part:, :] = total[NC * part :]


def finish_kernel(kinds, where, old_ref, mine_ref, came_ref, out, sums):
    half, width = came_ref.shape[0], old_ref.shape[1]
    core = where[4]
    sums[pl.ds(pl.multiple_of(core * half, half), half), :] = mine_ref[:half, :]
    sums[pl.ds(pl.multiple_of((1 - core) * half, half), half), :] = came_ref[...]
    blocks = width // LANES
    part = 2 * half // blocks
    lane = iota((part, LANES), 1)
    here = lane == iota((part, LANES), 0)
    count = jnp.sum(jnp.where(here, mine_ref[half : half + 1, :], 0.0), axis=1, keepdims=True)
    divisor = jnp.broadcast_to(count + 1.0, (part, LANES))
    rows = pl.ds(pl.multiple_of(where[5] * part, part), part)
    for k in range(blocks):
        at = slice(k * LANES, (k + 1) * LANES)
        out[:, at] = (sums[k * part : (k + 1) * part, :] + old_ref[rows, at]) / divisor
    count = jnp.where(lane == lax.rem(iota((part, LANES), 0), kinds), count, 0.0)
    line = iota((part, LANES), 0)
    tile = jnp.zeros((part, LANES), jnp.float32)
    for k in range(part // kinds):
        tile = jnp.where(line == k, jnp.sum(count[k * kinds : (k + 1) * kinds], axis=0, keepdims=True), tile)
    out[:, width:] = tile


def place_kernel(where, *rest):
    ins, (fresh_ref, count_ref) = rest[:-2], rest[-2:]
    part, width = ins[0].shape[0], fresh_ref.shape[1]
    kinds = count_ref.shape[1]
    for step, r in zip(TURNS, ins):
        q = lax.rem(where[5] - step + N, N)
        fresh_ref[pl.ds(pl.multiple_of(q * part, part), part), :] = r[:, :width]
        for k in range(part // kinds):
            line = r[k : k + 1, width : width + kinds]
            count_ref[pl.ds(q * (part // kinds) + k, 1), :] = line.astype(jnp.int32)


def per_device(pool_rows, sample_index, cluster_id, child_id, old_centroids):
    rows, width = pool_rows.shape
    block, kinds = old_centroids.shape[:2]
    owned = block // N
    most = 4 * rows // (block * N * NZ * NC)
    half = width // NC
    blocks = half // LANES
    chunk = N * NZ * NC * N * most // CHUNKS
    part = owned * kinds
    y, x, zh, zl, c = (lax.axis_index(a) for a in AXES)
    where = jnp.stack([x + (y - x) * c, y + (x - y) * c, zl, zh, c, y])

    def other_core(y, x, z, c):
        return y, x, z, 1 - c

    ints = jnp.stack([sample_index, cluster_id, child_id]).reshape(3, 1, rows)
    came_ints = permute(ints, other_core)
    came_pool = permute(pool_rows, other_core)
    slots = CHUNKS * chunk
    lines = [shape(slots // most, most), shape(slots // LANES, LANES)]
    own_lines = call(functools.partial(lines_kernel, most, owned, kinds), lines, [SMEM, VMEM], [where, ints])
    *came_lines, own_pool = call(
        functools.partial(pool_kernel, most, owned, kinds),
        [*lines, shape(rows, half, dtype=jnp.bfloat16)],
        [SMEM, VMEM, HBM],
        [where, came_ints, pltpu.with_memory_space_constraint(pool_rows, HBM)],
        [DMA],
    )
    came = []
    for moves in (RAW[:FIRST], RAW[FIRST:] + [(0, 0)]):
        packed = call(
            functools.partial(fill_kernel, [step * ZL + swap for step, swap in moves]),
            [shape(blocks * NC * chunk + TILE, LANES, dtype=jnp.bfloat16)] * len(moves),
            [SMEM] + [VMEM] * 6,
            [where, *own_lines, *came_lines, own_pool, came_pool],
            [VMEM((NC, len(moves) * chunk, rows), jnp.bfloat16)],
        )
        came += [permute(p, raw_move(*move)) if any(move) else p for p, move in zip(packed, moves)]
    segments = N * ZH * NC * part
    sums = [shape(segments, half), shape(chunk // LANES, TILE, segments * LANES // chunk)]
    early = call(functools.partial(early_kernel, most, part), sums, [VMEM] * EARLY, came[:EARLY])
    pieces = call(
        functools.partial(late_kernel, most, part),
        [shape(blocks * segments // N + TILE, LANES)] * N,
        [VMEM] * (2 + CHUNKS - EARLY),
        [*early, *came[EARLY:]],
    )
    pieces = [pieces[0]] + [permute(p, cross_move(t)) for t, p in zip(TURNS[1:], pieces[1:])]
    pieces = call(cross_kernel, [shape(blocks * NC * part + TILE, LANES)] * ZH, [VMEM] * N, pieces)
    pieces = [pieces[0]] + [
        permute(p, lambda y, x, z, c, t=t: (y, x, z + ZL * t, c)) for t, p in zip(DEEP[1:], pieces[1:])
    ]
    other, mine = call(
        functools.partial(depth_kernel, part),
        [shape(blocks * part, LANES), shape(blocks * part + TILE, LANES)],
        [VMEM] * ZH,
        pieces,
    )
    fresh = call(
        functools.partial(finish_kernel, kinds),
        shape(part, width + LANES),
        [SMEM, VMEM, VMEM, VMEM],
        [where, old_centroids.reshape(block * kinds, width), mine, permute(other, other_core)],
        [VMEM((NC * blocks * part, LANES), jnp.float32)],
    )
    quarters = [fresh] + [permute(fresh, lambda y, x, z, c, t=t: (y + t, x, z, c)) for t in TURNS[1:]]
    centroids, counts = call(
        place_kernel,
        [shape(block * kinds, width), shape(block, kinds, dtype=jnp.int32)],
        [SMEM] + [VMEM] * N,
        [where, *quarters],
    )
    return centroids.reshape(block, kinds, width), counts


def solution(mesh):
    fine = Mesh(mesh.devices.reshape(SIZES), AXES)
    dev = ("x", "zh", "zl", "c")
    placed = (P(AXES, None), P(AXES), P(AXES), P(AXES), P(dev, None, None))

    return jax.shard_map(
        per_device,
        mesh=fine,
        in_specs=placed,
        out_specs=(P(dev, None, None), P(dev, None)),
        check_vma=False,
    )
```

profile of v0, /device:TPU:36, one launch (start us, length us, event | category | flops | bytes accessed | tf_op | source)
XLA Modules:
  0.0 77.6 jit_solution(8921777514973039217)
XLA Ops:
  0.6 0.1 collective-permute-start.1
  0.7 0.7 pad_add_fusion
  1.5 0.6 collective-permute-start
  2.1 0.1 stack.39.where
  2.2 1.5 %shard_map.68 = (f32[256,8]{1,0:T(8,128)S(1)}, f32[16,128]{1,0:T(8,128)S(1)}) custom-call(s32[6]{0:T(128)S(1)} %stack.39.where, s32[3,1,1024]{2,1,0:T(1,128)S(1)} %reshape.14.ints_ref), custom_call_target="tpu_custom_call" | custom-call | tf_op jit(solution)/shard_map/pallas_call | solution.py:73
  3.7 1.4 %collective-permute-done.ints_ref = s32[3,1,1024]{2,1,0:T(1,128)S(1)} collective-permute-done((s32[3,1,1024]{2,1,0:T(1,128)S(1)}, s32[3,1,1024]{2,1,0:T(1,128)S(1)}, u32[]{:S(2)}, u32[]{:S(2)}) %collective-permute-start) | collective-permute-done | bytes 12320 | tf_op jit(solution)/shard_map/ppermute | solution.py:40
  5.1 2.6 %shard_map.69 = (f32[256,8]{1,0:T(8,128)S(1)}, f32[16,128]{1,0:T(8,128)S(1)}, bf16[1024,512]{1,0:T(8,128)(2,1)S(1)}) custom-call(s32[6]{0:T(128)S(1)} %stack.39.where, s32[3,1,1024]{2,1,0:T(1,128)S(1)} %collective-permute-done.ints_ref, bf16[1024,1024]{1,0:T(8,128)(2,1)} %pool_hbm.1), custom_call_target="tpu_custom_call" | custom-call | tf_op jit(solution)/shard_map/pallas_call | solution.py:73
  7.8 0.0 collective-permute-done.1.came_pool
  7.8 2.4 %shard_map.70 = (bf16[2056,128]{1,0:T(8,128)(2,1)S(1)}, bf16[2056,128]{1,0:T(8,128)(2,1)S(1)}, bf16[2056,128]{1,0:T(8,128)(2,1)S(1)}) custom-call(s32[6]{0:T(128)S(1)} %stack.39.where, f32[256,8]{1,0:T(8,128)S(1)} %get-tuple-element.29.own_source, f32[16,128]{1,0:T(8,128)S(1)} %get-tuple-element.30.own_label, f32[256,8]{1,0:T(8,128)S(1)} %get-tuple-element.31.came_source, ...), custom_call_target="tpu_custom_call" | custom-call | tf_op jit(solution)/shard_map/pallas_call | solution.py:73
  10.2 1.8 %collective-permute-start.2 = (bf16[2056,128]{1,0:T(8,128)(2,1)S(1)}, bf16[2056,128]{1,0:T(8,128)(2,1)S(1)}, u32[]{:S(2)}, u32[]{:S(2)}) collective-permute-start(bf16[2056,128]{1,0:T(8,128)(2,1)S(1)} %get-tuple-element.34), channel_id=1, source_target_pairs={{0,34},{1,143},{2,32},{3,133},{4,38},{5,131},{6,36},{7,137},{8,42}... | collective-permute-start | bytes 1579016 | tf_op jit(solution)/shard_map/ppermute | solution.py:40
  12.0 1.3 %collective-permute-start.3 = (bf16[2056,128]{1,0:T(8,128)(2,1)S(1)}, bf16[2056,128]{1,0:T(8,128)(2,1)S(1)}, u32[]{:S(2)}, u32[]{:S(2)}) collective-permute-start(bf16[2056,128]{1,0:T(8,128)(2,1)S(1)} %get-tuple-element.35), channel_id=1, source_target_pairs={{0,32},{1,129},{2,34},{3,131},{4,36},{5,133},{6,38},{7,135},{8,40}... | collective-permute-start | bytes 1579016 | tf_op jit(solution)/shard_map/ppermute | solution.py:40
  13.3 1.9 %collective-permute-start.4 = (bf16[2056,128]{1,0:T(8,128)(2,1)S(1)}, bf16[2056,128]{1,0:T(8,128)(2,1)S(1)}, u32[]{:S(2)}, u32[]{:S(2)}) collective-permute-start(bf16[2056,128]{1,0:T(8,128)(2,1)S(1)} %get-tuple-element.36), channel_id=1, source_target_pairs={{0,2},{1,15},{2,0},{3,5},{4,6},{5,3},{6,4},{7,9},{8,10},{9,7},{10,... | collective-permute-start | bytes 1579016 | tf_op jit(solution)/shard_map/ppermute | solution.py:40
  15.2 3.5 %shard_map.71 = (bf16[2056,128]{1,0:T(8,128)(2,1)S(1)}, bf16[2056,128]{1,0:T(8,128)(2,1)S(1)}, bf16[2056,128]{1,0:T(8,128)(2,1)S(1)}, bf16[2056,128]{1,0:T(8,128)(2,1)S(1)}, bf16[2056,128]{1,0:T(8,128)(2,1)S(1)}) custom-call(s32[6]{0:T(128)S(1)} %stack.39.where, f32[256,8]{1,0:T(8,128)S(1)} %get-tuple-element.29.own_source, ...), custom_call_target="tpu_custom_call" | custom-call | tf_op jit(solution)/shard_map/pallas_call | solution.py:73
  18.7 0.8 %collective-permute-start.5 = (bf16[2056,128]{1,0:T(8,128)(2,1)S(1)}, bf16[2056,128]{1,0:T(8,128)(2,1)S(1)}, u32[]{:S(2)}, u32[]{:S(2)}) collective-permute-start(bf16[2056,128]{1,0:T(8,128)(2,1)S(1)} %get-tuple-element.37), channel_id=1, source_target_pairs={{0,18},{1,79},{2,16},{3,69},{4,22},{5,67},{6,20},{7,73},{8,26},{9,... | collective-permute-start | bytes 1579016 | tf_op jit(solution)/shard_map/ppermute | solution.py:40
  19.6 0.8 %collective-permute-start.6 = (bf16[2056,128]{1,0:T(8,128)(2,1)S(1)}, bf16[2056,128]{1,0:T(8,128)(2,1)S(1)}, u32[]{:S(2)}, u32[]{:S(2)}) collective-permute-start(bf16[2056,128]{1,0:T(8,128)(2,1)S(1)} %get-tuple-element.40), channel_id=1, source_target_pairs={{0,48},{1,193},{2,50},{3,195},{4,52},{5,197},{6,54},{7,199},{8,56}... | collective-permute-start | bytes 1579016 | tf_op jit(solution)/shard_map/ppermute | solution.py:40
  20.4 1.6 %collective-permute-done.2.rest_0_ = bf16[2056,128]{1,0:T(8,128)(2,1)S(1)} collective-permute-done((bf16[2056,128]{1,0:T(8,128)(2,1)S(1)}, bf16[2056,128]{1,0:T(8,128)(2,1)S(1)}, u32[]{:S(2)}, u32[]{:S(2)}) %collective-permute-start.2) | collective-permute-done | bytes 526368 | tf_op jit(solution)/shard_map/ppermute | solution.py:40
  22.0 0.3 collective-permute-start.7
  22.3 6.0 %collective-permute-done.3.rest_1_ = bf16[2056,128]{1,0:T(8,128)(2,1)S(1)} collective-permute-done((bf16[2056,128]{1,0:T(8,128)(2,1)S(1)}, bf16[2056,128]{1,0:T(8,128)(2,1)S(1)}, u32[]{:S(2)}, u32[]{:S(2)}) %collective-permute-start.3) | collective-permute-done | bytes 526368 | tf_op jit(solution)/shard_map/ppermute | solution.py:40
  28.3 0.5 collective-permute-start.8
  28.8 0.0 collective-permute-done.4.rest_2_
  28.8 4.4 %collective-permute-done.5.rest_3_ = bf16[2056,128]{1,0:T(8,128)(2,1)S(1)} collective-permute-done((bf16[2056,128]{1,0:T(8,128)(2,1)S(1)}, bf16[2056,128]{1,0:T(8,128)(2,1)S(1)}, u32[]{:S(2)}, u32[]{:S(2)}) %collective-permute-start.5) | collective-permute-done | bytes 526368 | tf_op jit(solution)/shard_map/ppermute | solution.py:40
  33.2 1.0 %shard_map.72 = (f32[512,512]{1,0:T(8,128)S(1)}, f32[2,8,256]{2,1,0:T(8,128)S(1)}) custom-call(bf16[2056,128]{1,0:T(8,128)(2,1)S(1)} %collective-permute-done.2.rest_0_, bf16[2056,128]{1,0:T(8,128)(2,1)S(1)} %collective-permute-done.3.rest_1_, bf16[2056,128]{1,0:T(8,128)(2,1)S(1)} %collective-permute-done.4.rest_2_, ...), custom_call_target="tpu_custom_call" | custom-call | tf_op jit(solution)/shard_map/pallas_call | solution.py:73
  34.2 2.6 %collective-permute-done.6.rest_0_ = bf16[2056,128]{1,0:T(8,128)(2,1)S(1)} collective-permute-done((bf16[2056,128]{1,0:T(8,128)(2,1)S(1)}, bf16[2056,128]{1,0:T(8,128)(2,1)S(1)}, u32[]{:S(2)}, u32[]{:S(2)}) %collective-permute-start.6) | collective-permute-done | bytes 526368 | tf_op jit(solution)/shard_map/ppermute | solution.py:40
  36.8 1.1 %collective-permute-done.7.rest_1_ = bf16[2056,128]{1,0:T(8,128)(2,1)S(1)} collective-permute-done((bf16[2056,128]{1,0:T(8,128)(2,1)S(1)}, bf16[2056,128]{1,0:T(8,128)(2,1)S(1)}, u32[]{:S(2)}, u32[]{:S(2)}) %collective-permute-start.7) | collective-permute-done | bytes 526368 | tf_op jit(solution)/shard_map/ppermute | solution.py:40
  37.9 0.9 %collective-permute-done.8.rest_2_ = bf16[2056,128]{1,0:T(8,128)(2,1)S(1)} collective-permute-done((bf16[2056,128]{1,0:T(8,128)(2,1)S(1)}, bf16[2056,128]{1,0:T(8,128)(2,1)S(1)}, u32[]{:S(2)}, u32[]{:S(2)}) %collective-permute-start.8) | collective-permute-done | bytes 526368 | tf_op jit(solution)/shard_map/ppermute | solution.py:40
  38.8 0.0 copy-start
  38.8 0.9 %shard_map.73 = (f32[520,128]{1,0:T(8,128)S(1)}, f32[520,128]{1,0:T(8,128)S(1)}, f32[520,128]{1,0:T(8,128)S(1)}, f32[520,128]{1,0:T(8,128)S(1)}) custom-call(f32[512,512]{1,0:T(8,128)S(1)} %get-tuple-element.38.sum_ref, f32[2,8,256]{2,1,0:T(8,128)S(1)} %get-tuple-element.39.tally_ref, bf16[2056,128]{1,0:T(8,128)(2,1)S(1)} %collective-permute-done.6.rest_0_, ...), custom_call_target="tpu_custom_call" | custom-call | tf_op jit(solution)/shard_map/pallas_call | solution.py:73
  39.7 0.9 %collective-permute-start.9 = (f32[520,128]{1,0:T(8,128)S(1)}, f32[520,128]{1,0:T(8,128)S(1)}, u32[]{:S(2)}, u32[]{:S(2)}) collective-permute-start(f32[520,128]{1,0:T(8,128)S(1)} %get-tuple-element.45), channel_id=1, source_target_pairs={{0,64},{1,17},{2,66},{3,19},{4,68},{5,21},{6,70},{7,23},{8,72},{9,... | collective-permute-start | bytes 798728 | tf_op jit(solution)/shard_map/ppermute | solution.py:40
  40.6 2.5 %collective-permute-start.10 = (f32[520,128]{1,0:T(8,128)S(1)}, f32[520,128]{1,0:T(8,128)S(1)}, u32[]{:S(2)}, u32[]{:S(2)}) collective-permute-start(f32[520,128]{1,0:T(8,128)S(1)} %get-tuple-element.46), channel_id=1, source_target_pairs={{0,192},{1,49},{2,194},{3,51},{4,196},{5,53},{6,198},{7,55},{8,200... | collective-permute-start | bytes 798728 | tf_op jit(solution)/shard_map/ppermute | solution.py:40
  43.0 1.2 %collective-permute-start.11 = (f32[520,128]{1,0:T(8,128)S(1)}, f32[520,128]{1,0:T(8,128)S(1)}, u32[]{:S(2)}, u32[]{:S(2)}) collective-permute-start(f32[520,128]{1,0:T(8,128)S(1)} %get-tuple-element.47), channel_id=1, source_target_pairs={{0,128},{1,33},{2,130},{3,35},{4,132},{5,37},{6,134},{7,39},{8,136... | collective-permute-start | bytes 798728 | tf_op jit(solution)/shard_map/ppermute | solution.py:40
  44.2 3.2 %collective-permute-done.9.rest_1_ = f32[520,128]{1,0:T(8,128)S(1)} collective-permute-done((f32[520,128]{1,0:T(8,128)S(1)}, f32[520,128]{1,0:T(8,128)S(1)}, u32[]{:S(2)}, u32[]{:S(2)}) %collective-permute-start.9) | collective-permute-done | bytes 266272 | tf_op jit(solution)/shard_map/ppermute | solution.py:40
  47.4 2.4 %collective-permute-done.10.rest_2_ = f32[520,128]{1,0:T(8,128)S(1)} collective-permute-done((f32[520,128]{1,0:T(8,128)S(1)}, f32[520,128]{1,0:T(8,128)S(1)}, u32[]{:S(2)}, u32[]{:S(2)}) %collective-permute-start.10) | collective-permute-done | bytes 266272 | tf_op jit(solution)/shard_map/ppermute | solution.py:40
  49.9 1.1 %collective-permute-done.11.rest_3_ = f32[520,128]{1,0:T(8,128)S(1)} collective-permute-done((f32[520,128]{1,0:T(8,128)S(1)}, f32[520,128]{1,0:T(8,128)S(1)}, u32[]{:S(2)}, u32[]{:S(2)}) %collective-permute-start.11) | collective-permute-done | bytes 266272 | tf_op jit(solution)/shard_map/ppermute | solution.py:40
  51.0 0.1 shard_map.74
  51.0 6.9 %collective-permute-start.12 = (f32[136,128]{1,0:T(8,128)S(1)}, f32[136,128]{1,0:T(8,128)S(1)}, u32[]{:S(2)}, u32[]{:S(2)}) collective-permute-start(f32[136,128]{1,0:T(8,128)S(1)} %get-tuple-element.49), channel_id=1, source_target_pairs={{0,8},{1,9},{2,10},{3,11},{4,12},{5,13},{6,14},{7,15},{8,0},{9,1},... | collective-permute-start | bytes 208904 | tf_op jit(solution)/shard_map/ppermute | solution.py:40
  58.0 1.5 %collective-permute-start.13 = (f32[136,128]{1,0:T(8,128)S(1)}, f32[136,128]{1,0:T(8,128)S(1)}, u32[]{:S(2)}, u32[]{:S(2)}) collective-permute-start(f32[136,128]{1,0:T(8,128)S(1)} %get-tuple-element.50), channel_id=1, source_target_pairs={{0,4},{1,5},{2,6},{3,7},{4,8},{5,9},{6,10},{7,11},{8,12},{9,13},{1... | collective-permute-start | bytes 208904 | tf_op jit(solution)/shard_map/ppermute | solution.py:40
  59.5 2.7 %collective-permute-start.14 = (f32[136,128]{1,0:T(8,128)S(1)}, f32[136,128]{1,0:T(8,128)S(1)}, u32[]{:S(2)}, u32[]{:S(2)}) collective-permute-start(f32[136,128]{1,0:T(8,128)S(1)} %get-tuple-element.51), channel_id=1, source_target_pairs={{0,12},{1,13},{2,14},{3,15},{4,0},{5,1},{6,2},{7,3},{8,4},{9,5},{1... | collective-permute-start | bytes 208904 | tf_op jit(solution)/shard_map/ppermute | solution.py:40
  62.1 0.0 collective-permute-done.12.rest_1_
  62.1 3.0 %collective-permute-done.13.rest_2_ = f32[136,128]{1,0:T(8,128)S(1)} collective-permute-done((f32[136,128]{1,0:T(8,128)S(1)}, f32[136,128]{1,0:T(8,128)S(1)}, u32[]{:S(2)}, u32[]{:S(2)}) %collective-permute-start.13) | collective-permute-done | bytes 69664 | tf_op jit(solution)/shard_map/ppermute | solution.py:40
  65.1 0.1 collective-permute-done.14.rest_3_
  65.2 0.1 collective-permute-start.15
  65.3 1.2 %collective-permute-done.15.came_ref = f32[64,128]{1,0:T(8,128)S(1)} collective-permute-done((f32[64,128]{1,0:T(8,128)S(1)}, f32[64,128]{1,0:T(8,128)S(1)}, u32[]{:S(2)}, u32[]{:S(2)}) %collective-permute-start.15) | collective-permute-done | bytes 32800 | tf_op jit(solution)/shard_map/ppermute | solution.py:40
  66.5 0.0 copy-done
  66.5 0.6 shard_map.76.rest_0_
  67.2 1.5 %collective-permute-start.16 = (f32[16,1152]{1,0:T(8,128)S(1)}, f32[16,1152]{1,0:T(8,128)S(1)}, u32[]{:S(2)}, u32[]{:S(2)}) collective-permute-start(f32[16,1152]{1,0:T(8,128)S(1)} %shard_map.76.rest_0_), channel_id=1, source_target_pairs={{0,64},{1,65},{2,66},{3,67},{4,68},{5,69},{6,70},{7,71},{8,72},{9,... | collective-permute-start | bytes 221192 | tf_op jit(solution)/shard_map/ppermute | solution.py:40
  68.7 1.8 %collective-permute-start.17 = (f32[16,1152]{1,0:T(8,128)S(1)}, f32[16,1152]{1,0:T(8,128)S(1)}, u32[]{:S(2)}, u32[]{:S(2)}) collective-permute-start(f32[16,1152]{1,0:T(8,128)S(1)} %shard_map.76.rest_0_), channel_id=1, source_target_pairs={{0,192},{1,193},{2,194},{3,195},{4,196},{5,197},{6,198},{7,199},{8... | collective-permute-start | bytes 221192 | tf_op jit(solution)/shard_map/ppermute | solution.py:40
  70.5 0.4 collective-permute-start.18
  70.9 1.9 %collective-permute-done.16.rest_1_ = f32[16,1152]{1,0:T(8,128)S(1)} collective-permute-done((f32[16,1152]{1,0:T(8,128)S(1)}, f32[16,1152]{1,0:T(8,128)S(1)}, u32[]{:S(2)}, u32[]{:S(2)}) %collective-permute-start.16) | collective-permute-done | bytes 73760 | tf_op jit(solution)/shard_map/ppermute | solution.py:40
  72.8 0.9 %collective-permute-done.17.rest_2_ = f32[16,1152]{1,0:T(8,128)S(1)} collective-permute-done((f32[16,1152]{1,0:T(8,128)S(1)}, f32[16,1152]{1,0:T(8,128)S(1)}, u32[]{:S(2)}, u32[]{:S(2)}) %collective-permute-start.17) | collective-permute-done | bytes 73760 | tf_op jit(solution)/shard_map/ppermute | solution.py:40
  73.7 2.6 %collective-permute-done.18.rest_3_ = f32[16,1152]{1,0:T(8,128)S(1)} collective-permute-done((f32[16,1152]{1,0:T(8,128)S(1)}, f32[16,1152]{1,0:T(8,128)S(1)}, u32[]{:S(2)}, u32[]{:S(2)}) %collective-permute-start.18) | collective-permute-done | bytes 73760 | tf_op jit(solution)/shard_map/ppermute | solution.py:40
  76.3 1.3 %shard_map.77 = (f32[64,1024]{1,0:T(8,128)}, s32[8,8]{1,0:T(8,128)}) custom-call(s32[6]{0:T(128)S(1)} %stack.39.where, f32[16,1152]{1,0:T(8,128)S(1)} %shard_map.76.rest_0_, f32[16,1152]{1,0:T(8,128)S(1)} %collective-permute-done.16.rest_1_, f32[16,1152]{1,0:T(8,128)S(1)} %collective-permute-done.17.rest_2_, f32[16,1152]{1,0:T(8,128)S(1)} %collective-permute-done.18.rest_3_), custom_call_target="tpu_custom_call" | custom-call | tf_op jit(solution)/shard_map/pallas_call | solution.py:73
  (2 shorter events, 0.0 us)
Async XLA Ops:
  0.6 7.1 %collective-permute-start.1 = (bf16[1024,1024]{1,0:T(8,128)(2,1)}, bf16[1024,1024]{1,0:T(8,128)(2,1)S(1)}, u32[]{:S(2)}, u32[]{:S(2)}) collective-permute-start(bf16[1024,1024]{1,0:T(8,128)(2,1)} %pool_hbm.1), channel_id=1, source_target_pairs={{0,1},{1,0},{2,3},{3,2},{4,5},{5,4},{6,7},{7,6},{8,9},{9,8},{10,11... | collective-permute-start | bytes 6291464 | tf_op jit(solution)/shard_map/ppermute | solution.py:40
  1.5 3.6 %collective-permute-start = (s32[3,1,1024]{2,1,0:T(1,128)S(1)}, s32[3,1,1024]{2,1,0:T(1,128)S(1)}, u32[]{:S(2)}, u32[]{:S(2)}) collective-permute-start(s32[3,1,1024]{2,1,0:T(1,128)S(1)} %reshape.14.ints_ref), channel_id=1, source_target_pairs={{0,1},{1,0},{2,3},{3,2},{4,5},{5,4},{6,7},{7,6},{8,9},{9,8},{10,11... | collective-permute-start | bytes 36872 | tf_op jit(solution)/shard_map/ppermute | solution.py:40
  10.2 11.8 %collective-permute-start.2 = (bf16[2056,128]{1,0:T(8,128)(2,1)S(1)}, bf16[2056,128]{1,0:T(8,128)(2,1)S(1)}, u32[]{:S(2)}, u32[]{:S(2)}) collective-permute-start(bf16[2056,128]{1,0:T(8,128)(2,1)S(1)} %get-tuple-element.34), channel_id=1, source_target_pairs={{0,34},{1,143},{2,32},{3,133},{4,38},{5,131},{6,36},{7,137},{8,42}... | collective-permute-start | bytes 1579016 | tf_op jit(solution)/shard_map/ppermute | solution.py:40
  12.0 16.3 %collective-permute-start.3 = (bf16[2056,128]{1,0:T(8,128)(2,1)S(1)}, bf16[2056,128]{1,0:T(8,128)(2,1)S(1)}, u32[]{:S(2)}, u32[]{:S(2)}) collective-permute-start(bf16[2056,128]{1,0:T(8,128)(2,1)S(1)} %get-tuple-element.35), channel_id=1, source_target_pairs={{0,32},{1,129},{2,34},{3,131},{4,36},{5,133},{6,38},{7,135},{8,40}... | collective-permute-start | bytes 1579016 | tf_op jit(solution)/shard_map/ppermute | solution.py:40
  13.3 15.5 %collective-permute-start.4 = (bf16[2056,128]{1,0:T(8,128)(2,1)S(1)}, bf16[2056,128]{1,0:T(8,128)(2,1)S(1)}, u32[]{:S(2)}, u32[]{:S(2)}) collective-permute-start(bf16[2056,128]{1,0:T(8,128)(2,1)S(1)} %get-tuple-element.36), channel_id=1, source_target_pairs={{0,2},{1,15},{2,0},{3,5},{4,6},{5,3},{6,4},{7,9},{8,10},{9,7},{10,... | collective-permute-start | bytes 1579016 | tf_op jit(solution)/shard_map/ppermute | solution.py:40
  18.7 14.5 %collective-permute-start.5 = (bf16[2056,128]{1,0:T(8,128)(2,1)S(1)}, bf16[2056,128]{1,0:T(8,128)(2,1)S(1)}, u32[]{:S(2)}, u32[]{:S(2)}) collective-permute-start(bf16[2056,128]{1,0:T(8,128)(2,1)S(1)} %get-tuple-element.37), channel_id=1, source_target_pairs={{0,18},{1,79},{2,16},{3,69},{4,22},{5,67},{6,20},{7,73},{8,26},{9,... | collective-permute-start | bytes 1579016 | tf_op jit(solution)/shard_map/ppermute | solution.py:40
  19.6 17.3 %collective-permute-start.6 = (bf16[2056,128]{1,0:T(8,128)(2,1)S(1)}, bf16[2056,128]{1,0:T(8,128)(2,1)S(1)}, u32[]{:S(2)}, u32[]{:S(2)}) collective-permute-start(bf16[2056,128]{1,0:T(8,128)(2,1)S(1)} %get-tuple-element.40), channel_id=1, source_target_pairs={{0,48},{1,193},{2,50},{3,195},{4,52},{5,197},{6,54},{7,199},{8,56}... | collective-permute-start | bytes 1579016 | tf_op jit(solution)/shard_map/ppermute | solution.py:40
  22.0 15.9 %collective-permute-start.7 = (bf16[2056,128]{1,0:T(8,128)(2,1)S(1)}, bf16[2056,128]{1,0:T(8,128)(2,1)S(1)}, u32[]{:S(2)}, u32[]{:S(2)}) collective-permute-start(bf16[2056,128]{1,0:T(8,128)(2,1)S(1)} %get-tuple-element.41), channel_id=1, source_target_pairs={{0,50},{1,207},{2,48},{3,197},{4,54},{5,195},{6,52},{7,201},{8,58}... | collective-permute-start | bytes 1579016 | tf_op jit(solution)/shard_map/ppermute | solution.py:40
  28.3 10.5 %collective-permute-start.8 = (bf16[2056,128]{1,0:T(8,128)(2,1)S(1)}, bf16[2056,128]{1,0:T(8,128)(2,1)S(1)}, u32[]{:S(2)}, u32[]{:S(2)}) collective-permute-start(bf16[2056,128]{1,0:T(8,128)(2,1)S(1)} %get-tuple-element.42), channel_id=1, source_target_pairs={{0,16},{1,65},{2,18},{3,67},{4,20},{5,69},{6,22},{7,71},{8,24},{9,... | collective-permute-start | bytes 1579016 | tf_op jit(solution)/shard_map/ppermute | solution.py:40
  38.8 27.8 %copy-start = (f32[8,8,1024]{2,1,0:T(8,128)S(1)}, f32[8,8,1024]{2,1,0:T(8,128)}, u32[]{:S(2)}) copy-start(f32[8,8,1024]{2,1,0:T(8,128)} %param.9) | copy-start | bytes 786436
  39.7 7.7 %collective-permute-start.9 = (f32[520,128]{1,0:T(8,128)S(1)}, f32[520,128]{1,0:T(8,128)S(1)}, u32[]{:S(2)}, u32[]{:S(2)}) collective-permute-start(f32[520,128]{1,0:T(8,128)S(1)} %get-tuple-element.45), channel_id=1, source_target_pairs={{0,64},{1,17},{2,66},{3,19},{4,68},{5,21},{6,70},{7,23},{8,72},{9,... | collective-permute-start | bytes 798728 | tf_op jit(solution)/shard_map/ppermute | solution.py:40
  40.6 9.3 %collective-permute-start.10 = (f32[520,128]{1,0:T(8,128)S(1)}, f32[520,128]{1,0:T(8,128)S(1)}, u32[]{:S(2)}, u32[]{:S(2)}) collective-permute-start(f32[520,128]{1,0:T(8,128)S(1)} %get-tuple-element.46), channel_id=1, source_target_pairs={{0,192},{1,49},{2,194},{3,51},{4,196},{5,53},{6,198},{7,55},{8,200... | collective-permute-start | bytes 798728 | tf_op jit(solution)/shard_map/ppermute | solution.py:40
  43.0 7.9 %collective-permute-start.11 = (f32[520,128]{1,0:T(8,128)S(1)}, f32[520,128]{1,0:T(8,128)S(1)}, u32[]{:S(2)}, u32[]{:S(2)}) collective-permute-start(f32[520,128]{1,0:T(8,128)S(1)} %get-tuple-element.47), channel_id=1, source_target_pairs={{0,128},{1,33},{2,130},{3,35},{4,132},{5,37},{6,134},{7,39},{8,136... | collective-permute-start | bytes 798728 | tf_op jit(solution)/shard_map/ppermute | solution.py:40
  51.0 11.1 %collective-permute-start.12 = (f32[136,128]{1,0:T(8,128)S(1)}, f32[136,128]{1,0:T(8,128)S(1)}, u32[]{:S(2)}, u32[]{:S(2)}) collective-permute-start(f32[136,128]{1,0:T(8,128)S(1)} %get-tuple-element.49), channel_id=1, source_target_pairs={{0,8},{1,9},{2,10},{3,11},{4,12},{5,13},{6,14},{7,15},{8,0},{9,1},... | collective-permute-start | bytes 208904 | tf_op jit(solution)/shard_map/ppermute | solution.py:40
  58.0 7.2 %collective-permute-start.13 = (f32[136,128]{1,0:T(8,128)S(1)}, f32[136,128]{1,0:T(8,128)S(1)}, u32[]{:S(2)}, u32[]{:S(2)}) collective-permute-start(f32[136,128]{1,0:T(8,128)S(1)} %get-tuple-element.50), channel_id=1, source_target_pairs={{0,4},{1,5},{2,6},{3,7},{4,8},{5,9},{6,10},{7,11},{8,12},{9,13},{1... | collective-permute-start | bytes 208904 | tf_op jit(solution)/shard_map/ppermute | solution.py:40
  59.5 5.8 %collective-permute-start.14 = (f32[136,128]{1,0:T(8,128)S(1)}, f32[136,128]{1,0:T(8,128)S(1)}, u32[]{:S(2)}, u32[]{:S(2)}) collective-permute-start(f32[136,128]{1,0:T(8,128)S(1)} %get-tuple-element.51), channel_id=1, source_target_pairs={{0,12},{1,13},{2,14},{3,15},{4,0},{5,1},{6,2},{7,3},{8,4},{9,5},{1... | collective-permute-start | bytes 208904 | tf_op jit(solution)/shard_map/ppermute | solution.py:40
  65.2 1.3 %collective-permute-start.15 = (f32[64,128]{1,0:T(8,128)S(1)}, f32[64,128]{1,0:T(8,128)S(1)}, u32[]{:S(2)}, u32[]{:S(2)}) collective-permute-start(f32[64,128]{1,0:T(8,128)S(1)} %get-tuple-element.53), channel_id=1, source_target_pairs={{0,1},{1,0},{2,3},{3,2},{4,5},{5,4},{6,7},{7,6},{8,9},{9,8},{10,11... | collective-permute-start | bytes 98312 | tf_op jit(solution)/shard_map/ppermute | solution.py:40
  67.2 5.6 %collective-permute-start.16 = (f32[16,1152]{1,0:T(8,128)S(1)}, f32[16,1152]{1,0:T(8,128)S(1)}, u32[]{:S(2)}, u32[]{:S(2)}) collective-permute-start(f32[16,1152]{1,0:T(8,128)S(1)} %shard_map.76.rest_0_), channel_id=1, source_target_pairs={{0,64},{1,65},{2,66},{3,67},{4,68},{5,69},{6,70},{7,71},{8,72},{9,... | collective-permute-start | bytes 221192 | tf_op jit(solution)/shard_map/ppermute | solution.py:40
  68.7 5.1 %collective-permute-start.17 = (f32[16,1152]{1,0:T(8,128)S(1)}, f32[16,1152]{1,0:T(8,128)S(1)}, u32[]{:S(2)}, u32[]{:S(2)}) collective-permute-start(f32[16,1152]{1,0:T(8,128)S(1)} %shard_map.76.rest_0_), channel_id=1, source_target_pairs={{0,192},{1,193},{2,194},{3,195},{4,196},{5,197},{6,198},{7,199},{8... | collective-permute-start | bytes 221192 | tf_op jit(solution)/shard_map/ppermute | solution.py:40
  70.5 5.9 %collective-permute-start.18 = (f32[16,1152]{1,0:T(8,128)S(1)}, f32[16,1152]{1,0:T(8,128)S(1)}, u32[]{:S(2)}, u32[]{:S(2)}) collective-permute-start(f32[16,1152]{1,0:T(8,128)S(1)} %shard_map.76.rest_0_), channel_id=1, source_target_pairs={{0,128},{1,129},{2,130},{3,131},{4,132},{5,133},{6,134},{7,135},{8... | collective-permute-start | bytes 221192 | tf_op jit(solution)/shard_map/ppermute | solution.py:40
where the time goes:
time: 78.9 us; the launch traced here: 77.6 us
  waiting for transfers between devices  34.6 us (44%)
  starting transfers between devices  27.6 us (35%)
  Pallas kernels  13.9 us (18%)
    ppermute x19, waiting for transfers between devices, permute(): return lax.ppermute(value, AXES, pairs)  34.6 us
    ppermute x19, starting transfers between devices, permute(): return lax.ppermute(value, AXES, pairs)  27.6 us
    pallas_call x10, Pallas kernels, call(): pl.pallas_call(kernel, out_shape=outs, in_specs=[pl.BlockSpec(memory_spac...  13.9 us
  transfers between devices with their start and end apart: 19, of which 16 were waited for; matrix products, arithmetic and copies ran while one was open for 1% of the time, Pallas kernels for 11%

commit v1 on v0

--- a/solution.py
+++ b/solution.py
@@ -23,6 +23,7 @@
 
 RAW = [(2, 1), (2, 0), (0, 1), (1, 1), (3, 0), (3, 1), (1, 0)]
 FIRST = 3
+CROSS = [0, 2, 1, 3]
 DEEP = [0, 2, 1, 3]
 TURNS = [0, 1, 3, 2]
 EARLY = 4
@@ -217,7 +218,7 @@
         before = (sum_ref[h * segments : (h + 1) * segments, :], tally_ref[h])
         sums, count = add_up(most, kinds2, ins, h, before)
         for p in range(segments // part):
-            out = outs[TURNS.index(h * (segments // part) + p)]
+            out = outs[CROSS.index(h * (segments // part) + p)]
             for k in range(blocks):
                 out[k * part : (k + 1) * part, :] = sums[p * part : (p + 1) * part, k * LANES : (k + 1) * LANES]
             out[blocks * part :, :] = count[:, p * part : (p + 1) * part]
@@ -329,7 +330,7 @@
         [VMEM] * (2 + CHUNKS - EARLY),
         [*early, *came[EARLY:]],
     )
-    pieces = [pieces[0]] + [permute(p, cross_move(t)) for t, p in zip(TURNS[1:], pieces[1:])]
+    pieces = [pieces[0]] + [permute(p, cross_move(t)) for t, p in zip(CROSS[1:], pieces[1:])]
     pieces = call(cross_kernel, [shape(blocks * NC * part + TILE, LANES)] * ZH, [VMEM] * N, pieces)
     pieces = [pieces[0]] + [
         permute(p, lambda y, x, z, c, t=t: (y, x, z + ZL * t, c)) for t, p in zip(DEEP[1:], pieces[1:])

time: 78.9 us -> 78.4 us (level)
  waiting for transfers between devices: 34.6 us -> 32.2 us
  starting transfers between devices: 27.6 us -> 29.3 us
    ppermute x19, waiting for transfers between devices: 34.6 us -> 32.2 us  [permute(): return lax.ppermute(value, AXES, pairs)]
    ppermute x19, starting transfers between devices: 27.6 us -> 29.3 us  [permute(): return lax.ppermute(value, AXES, pairs)]
  transfers between devices with their start and end apart: 19 -> 19, of which waited for: 16 -> 15; matrix products, arithmetic and copies ran while one was open for 1% -> 1% of each run, Pallas kernels for 11% -> 11%
where the time goes in v1:
time: 78.4 us; the launch traced here: 77 us
  waiting for transfers between devices  32.2 us (41%)
  starting transfers between devices  29.3 us (37%)
  Pallas kernels  13.9 us (18%)
    ppermute x19, waiting for transfers between devices, permute(): return lax.ppermute(value, AXES, pairs)  32.2 us
    ppermute x19, starting transfers between devices, permute(): return lax.ppermute(value, AXES, pairs)  29.3 us
    pallas_call x10, Pallas kernels, call(): pl.pallas_call(kernel, out_shape=outs, in_specs=[pl.BlockSpec(memory_spac...  13.9 us
  transfers between devices with their start and end apart: 19, of which 15 were waited for; matrix products, arithmetic and copies ran while one was open for 1% of the time, Pallas kernels for 11%

profile of v1, /device:TPU:36, one launch (start us, length us, event | category | flops | bytes accessed | tf_op | source)
XLA Modules:
  0.0 77.0 jit_solution(5304421779003790391)
XLA Ops:
  0.6 0.1 collective-permute-start.1
  0.7 0.7 pad_add_fusion
  1.5 0.6 collective-permute-start
  2.1 0.1 stack.39.where
  2.2 1.5 %shard_map.68 = (f32[256,8]{1,0:T(8,128)S(1)}, f32[16,128]{1,0:T(8,128)S(1)}) custom-call(s32[6]{0:T(128)S(1)} %stack.39.where, s32[3,1,1024]{2,1,0:T(1,128)S(1)} %reshape.14.ints_ref), custom_call_target="tpu_custom_call" | custom-call | tf_op jit(solution)/shard_map/pallas_call | solution.py:74
  3.7 1.4 %collective-permute-done.ints_ref = s32[3,1,1024]{2,1,0:T(1,128)S(1)} collective-permute-done((s32[3,1,1024]{2,1,0:T(1,128)S(1)}, s32[3,1,1024]{2,1,0:T(1,128)S(1)}, u32[]{:S(2)}, u32[]{:S(2)}) %collective-permute-start) | collective-permute-done | bytes 12320 | tf_op jit(solution)/shard_map/ppermute | solution.py:41
  5.1 2.6 %shard_map.69 = (f32[256,8]{1,0:T(8,128)S(1)}, f32[16,128]{1,0:T(8,128)S(1)}, bf16[1024,512]{1,0:T(8,128)(2,1)S(1)}) custom-call(s32[6]{0:T(128)S(1)} %stack.39.where, s32[3,1,1024]{2,1,0:T(1,128)S(1)} %collective-permute-done.ints_ref, bf16[1024,1024]{1,0:T(8,128)(2,1)} %pool_hbm.1), custom_call_target="tpu_custom_call" | custom-call | tf_op jit(solution)/shard_map/pallas_call | solution.py:74
  7.8 0.0 collective-permute-done.1.came_pool
  7.8 2.4 %shard_map.70 = (bf16[2056,128]{1,0:T(8,128)(2,1)S(1)}, bf16[2056,128]{1,0:T(8,128)(2,1)S(1)}, bf16[2056,128]{1,0:T(8,128)(2,1)S(1)}) custom-call(s32[6]{0:T(128)S(1)} %stack.39.where, f32[256,8]{1,0:T(8,128)S(1)} %get-tuple-element.29.own_source, f32[16,128]{1,0:T(8,128)S(1)} %get-tuple-element.30.own_label, f32[256,8]{1,0:T(8,128)S(1)} %get-tuple-element.31.came_source, ...), custom_call_target="tpu_custom_call" | custom-call | tf_op jit(solution)/shard_map/pallas_call | solution.py:74
  10.2 1.8 %collective-permute-start.2 = (bf16[2056,128]{1,0:T(8,128)(2,1)S(1)}, bf16[2056,128]{1,0:T(8,128)(2,1)S(1)}, u32[]{:S(2)}, u32[]{:S(2)}) collective-permute-start(bf16[2056,128]{1,0:T(8,128)(2,1)S(1)} %get-tuple-element.34), channel_id=1, source_target_pairs={{0,34},{1,143},{2,32},{3,133},{4,38},{5,131},{6,36},{7,137},{8,42}... | collective-permute-start | bytes 1579016 | tf_op jit(solution)/shard_map/ppermute | solution.py:41
  12.0 1.3 %collective-permute-start.3 = (bf16[2056,128]{1,0:T(8,128)(2,1)S(1)}, bf16[2056,128]{1,0:T(8,128)(2,1)S(1)}, u32[]{:S(2)}, u32[]{:S(2)}) collective-permute-start(bf16[2056,128]{1,0:T(8,128)(2,1)S(1)} %get-tuple-element.35), channel_id=1, source_target_pairs={{0,32},{1,129},{2,34},{3,131},{4,36},{5,133},{6,38},{7,135},{8,40}... | collective-permute-start | bytes 1579016 | tf_op jit(solution)/shard_map/ppermute | solution.py:41
  13.3 1.9 %collective-permute-start.4 = (bf16[2056,128]{1,0:T(8,128)(2,1)S(1)}, bf16[2056,128]{1,0:T(8,128)(2,1)S(1)}, u32[]{:S(2)}, u32[]{:S(2)}) collective-permute-start(bf16[2056,128]{1,0:T(8,128)(2,1)S(1)} %get-tuple-element.36), channel_id=1, source_target_pairs={{0,2},{1,15},{2,0},{3,5},{4,6},{5,3},{6,4},{7,9},{8,10},{9,7},{10,... | collective-permute-start | bytes 1579016 | tf_op jit(solution)/shard_map/ppermute | solution.py:41
  15.2 3.5 %shard_map.71 = (bf16[2056,128]{1,0:T(8,128)(2,1)S(1)}, bf16[2056,128]{1,0:T(8,128)(2,1)S(1)}, bf16[2056,128]{1,0:T(8,128)(2,1)S(1)}, bf16[2056,128]{1,0:T(8,128)(2,1)S(1)}, bf16[2056,128]{1,0:T(8,128)(2,1)S(1)}) custom-call(s32[6]{0:T(128)S(1)} %stack.39.where, f32[256,8]{1,0:T(8,128)S(1)} %get-tuple-element.29.own_source, ...), custom_call_target="tpu_custom_call" | custom-call | tf_op jit(solution)/shard_map/pallas_call | solution.py:74
  18.7 0.8 %collective-permute-start.5 = (bf16[2056,128]{1,0:T(8,128)(2,1)S(1)}, bf16[2056,128]{1,0:T(8,128)(2,1)S(1)}, u32[]{:S(2)}, u32[]{:S(2)}) collective-permute-start(bf16[2056,128]{1,0:T(8,128)(2,1)S(1)} %get-tuple-element.37), channel_id=1, source_target_pairs={{0,18},{1,79},{2,16},{3,69},{4,22},{5,67},{6,20},{7,73},{8,26},{9,... | collective-permute-start | bytes 1579016 | tf_op jit(solution)/shard_map/ppermute | solution.py:41
  19.6 0.8 %collective-permute-start.6 = (bf16[2056,128]{1,0:T(8,128)(2,1)S(1)}, bf16[2056,128]{1,0:T(8,128)(2,1)S(1)}, u32[]{:S(2)}, u32[]{:S(2)}) collective-permute-start(bf16[2056,128]{1,0:T(8,128)(2,1)S(1)} %get-tuple-element.40), channel_id=1, source_target_pairs={{0,48},{1,193},{2,50},{3,195},{4,52},{5,197},{6,54},{7,199},{8,56}... | collective-permute-start | bytes 1579016 | tf_op jit(solution)/shard_map/ppermute | solution.py:41
  20.4 1.6 %collective-permute-done.2.rest_0_ = bf16[2056,128]{1,0:T(8,128)(2,1)S(1)} collective-permute-done((bf16[2056,128]{1,0:T(8,128)(2,1)S(1)}, bf16[2056,128]{1,0:T(8,128)(2,1)S(1)}, u32[]{:S(2)}, u32[]{:S(2)}) %collective-permute-start.2) | collective-permute-done | bytes 526368 | tf_op jit(solution)/shard_map/ppermute | solution.py:41
  22.0 0.3 collective-permute-start.7
  22.3 6.0 %collective-permute-done.3.rest_1_ = bf16[2056,128]{1,0:T(8,128)(2,1)S(1)} collective-permute-done((bf16[2056,128]{1,0:T(8,128)(2,1)S(1)}, bf16[2056,128]{1,0:T(8,128)(2,1)S(1)}, u32[]{:S(2)}, u32[]{:S(2)}) %collective-permute-start.3) | collective-permute-done | bytes 526368 | tf_op jit(solution)/shard_map/ppermute | solution.py:41
  28.3 0.5 collective-permute-start.8
  28.8 0.0 collective-permute-done.4.rest_2_
  28.8 4.4 %collective-permute-done.5.rest_3_ = bf16[2056,128]{1,0:T(8,128)(2,1)S(1)} collective-permute-done((bf16[2056,128]{1,0:T(8,128)(2,1)S(1)}, bf16[2056,128]{1,0:T(8,128)(2,1)S(1)}, u32[]{:S(2)}, u32[]{:S(2)}) %collective-permute-start.5) | collective-permute-done | bytes 526368 | tf_op jit(solution)/shard_map/ppermute | solution.py:41
  33.2 1.0 %shard_map.72 = (f32[512,512]{1,0:T(8,128)S(1)}, f32[2,8,256]{2,1,0:T(8,128)S(1)}) custom-call(bf16[2056,128]{1,0:T(8,128)(2,1)S(1)} %collective-permute-done.2.rest_0_, bf16[2056,128]{1,0:T(8,128)(2,1)S(1)} %collective-permute-done.3.rest_1_, bf16[2056,128]{1,0:T(8,128)(2,1)S(1)} %collective-permute-done.4.rest_2_, ...), custom_call_target="tpu_custom_call" | custom-call | tf_op jit(solution)/shard_map/pallas_call | solution.py:74
  34.2 2.6 %collective-permute-done.6.rest_0_ = bf16[2056,128]{1,0:T(8,128)(2,1)S(1)} collective-permute-done((bf16[2056,128]{1,0:T(8,128)(2,1)S(1)}, bf16[2056,128]{1,0:T(8,128)(2,1)S(1)}, u32[]{:S(2)}, u32[]{:S(2)}) %collective-permute-start.6) | collective-permute-done | bytes 526368 | tf_op jit(solution)/shard_map/ppermute | solution.py:41
  36.8 1.1 %collective-permute-done.7.rest_1_ = bf16[2056,128]{1,0:T(8,128)(2,1)S(1)} collective-permute-done((bf16[2056,128]{1,0:T(8,128)(2,1)S(1)}, bf16[2056,128]{1,0:T(8,128)(2,1)S(1)}, u32[]{:S(2)}, u32[]{:S(2)}) %collective-permute-start.7) | collective-permute-done | bytes 526368 | tf_op jit(solution)/shard_map/ppermute | solution.py:41
  37.9 0.9 %collective-permute-done.8.rest_2_ = bf16[2056,128]{1,0:T(8,128)(2,1)S(1)} collective-permute-done((bf16[2056,128]{1,0:T(8,128)(2,1)S(1)}, bf16[2056,128]{1,0:T(8,128)(2,1)S(1)}, u32[]{:S(2)}, u32[]{:S(2)}) %collective-permute-start.8) | collective-permute-done | bytes 526368 | tf_op jit(solution)/shard_map/ppermute | solution.py:41
  38.8 0.0 copy-start
  38.8 0.9 %shard_map.73 = (f32[520,128]{1,0:T(8,128)S(1)}, f32[520,128]{1,0:T(8,128)S(1)}, f32[520,128]{1,0:T(8,128)S(1)}, f32[520,128]{1,0:T(8,128)S(1)}) custom-call(f32[512,512]{1,0:T(8,128)S(1)} %get-tuple-element.38.sum_ref, f32[2,8,256]{2,1,0:T(8,128)S(1)} %get-tuple-element.39.tally_ref, bf16[2056,128]{1,0:T(8,128)(2,1)S(1)} %collective-permute-done.6.rest_0_, ...), custom_call_target="tpu_custom_call" | custom-call | tf_op jit(solution)/shard_map/pallas_call | solution.py:74
  39.7 2.5 %collective-permute-start.9 = (f32[520,128]{1,0:T(8,128)S(1)}, f32[520,128]{1,0:T(8,128)S(1)}, u32[]{:S(2)}, u32[]{:S(2)}) collective-permute-start(f32[520,128]{1,0:T(8,128)S(1)} %get-tuple-element.45), channel_id=1, source_target_pairs={{0,128},{1,33},{2,130},{3,35},{4,132},{5,37},{6,134},{7,39},{8,136... | collective-permute-start | bytes 798728 | tf_op jit(solution)/shard_map/ppermute | solution.py:41
  42.2 0.7 collective-permute-start.10
  42.9 2.6 %collective-permute-start.11 = (f32[520,128]{1,0:T(8,128)S(1)}, f32[520,128]{1,0:T(8,128)S(1)}, u32[]{:S(2)}, u32[]{:S(2)}) collective-permute-start(f32[520,128]{1,0:T(8,128)S(1)} %get-tuple-element.47), channel_id=1, source_target_pairs={{0,192},{1,49},{2,194},{3,51},{4,196},{5,53},{6,198},{7,55},{8,200... | collective-permute-start | bytes 798728 | tf_op jit(solution)/shard_map/ppermute | solution.py:41
  45.4 2.4 %collective-permute-done.9.rest_1_ = f32[520,128]{1,0:T(8,128)S(1)} collective-permute-done((f32[520,128]{1,0:T(8,128)S(1)}, f32[520,128]{1,0:T(8,128)S(1)}, u32[]{:S(2)}, u32[]{:S(2)}) %collective-permute-start.9) | collective-permute-done | bytes 266272 | tf_op jit(solution)/shard_map/ppermute | solution.py:41
  47.8 2.8 %collective-permute-done.10.rest_2_ = f32[520,128]{1,0:T(8,128)S(1)} collective-permute-done((f32[520,128]{1,0:T(8,128)S(1)}, f32[520,128]{1,0:T(8,128)S(1)}, u32[]{:S(2)}, u32[]{:S(2)}) %collective-permute-start.10) | collective-permute-done | bytes 266272 | tf_op jit(solution)/shard_map/ppermute | solution.py:41
  50.6 0.0 collective-permute-done.11.rest_3_
  50.6 0.1 shard_map.74
  50.7 6.7 %collective-permute-start.12 = (f32[136,128]{1,0:T(8,128)S(1)}, f32[136,128]{1,0:T(8,128)S(1)}, u32[]{:S(2)}, u32[]{:S(2)}) collective-permute-start(f32[136,128]{1,0:T(8,128)S(1)} %get-tuple-element.49), channel_id=1, source_target_pairs={{0,8},{1,9},{2,10},{3,11},{4,12},{5,13},{6,14},{7,15},{8,0},{9,1},... | collective-permute-start | bytes 208904 | tf_op jit(solution)/shard_map/ppermute | solution.py:41
  57.4 1.5 %collective-permute-start.13 = (f32[136,128]{1,0:T(8,128)S(1)}, f32[136,128]{1,0:T(8,128)S(1)}, u32[]{:S(2)}, u32[]{:S(2)}) collective-permute-start(f32[136,128]{1,0:T(8,128)S(1)} %get-tuple-element.50), channel_id=1, source_target_pairs={{0,4},{1,5},{2,6},{3,7},{4,8},{5,9},{6,10},{7,11},{8,12},{9,13},{1... | collective-permute-start | bytes 208904 | tf_op jit(solution)/shard_map/ppermute | solution.py:41
  58.9 2.7 %collective-permute-start.14 = (f32[136,128]{1,0:T(8,128)S(1)}, f32[136,128]{1,0:T(8,128)S(1)}, u32[]{:S(2)}, u32[]{:S(2)}) collective-permute-start(f32[136,128]{1,0:T(8,128)S(1)} %get-tuple-element.51), channel_id=1, source_target_pairs={{0,12},{1,13},{2,14},{3,15},{4,0},{5,1},{6,2},{7,3},{8,4},{9,5},{1... | collective-permute-start | bytes 208904 | tf_op jit(solution)/shard_map/ppermute | solution.py:41
  61.5 0.0 collective-permute-done.12.rest_1_
  61.5 3.0 %collective-permute-done.13.rest_2_ = f32[136,128]{1,0:T(8,128)S(1)} collective-permute-done((f32[136,128]{1,0:T(8,128)S(1)}, f32[136,128]{1,0:T(8,128)S(1)}, u32[]{:S(2)}, u32[]{:S(2)}) %collective-permute-start.13) | collective-permute-done | bytes 69664 | tf_op jit(solution)/shard_map/ppermute | solution.py:41
  64.6 0.1 collective-permute-done.14.rest_3_
  64.6 0.1 collective-permute-start.15
  64.7 1.2 %collective-permute-done.15.came_ref = f32[64,128]{1,0:T(8,128)S(1)} collective-permute-done((f32[64,128]{1,0:T(8,128)S(1)}, f32[64,128]{1,0:T(8,128)S(1)}, u32[]{:S(2)}, u32[]{:S(2)}) %collective-permute-start.15) | collective-permute-done | bytes 32800 | tf_op jit(solution)/shard_map/ppermute | solution.py:41
  65.9 0.0 copy-done
  65.9 0.6 shard_map.76.rest_0_
  66.6 1.6 %collective-permute-start.16 = (f32[16,1152]{1,0:T(8,128)S(1)}, f32[16,1152]{1,0:T(8,128)S(1)}, u32[]{:S(2)}, u32[]{:S(2)}) collective-permute-start(f32[16,1152]{1,0:T(8,128)S(1)} %shard_map.76.rest_0_), channel_id=1, source_target_pairs={{0,64},{1,65},{2,66},{3,67},{4,68},{5,69},{6,70},{7,71},{8,72},{9,... | collective-permute-start | bytes 221192 | tf_op jit(solution)/shard_map/ppermute | solution.py:41
  68.1 1.7 %collective-permute-start.17 = (f32[16,1152]{1,0:T(8,128)S(1)}, f32[16,1152]{1,0:T(8,128)S(1)}, u32[]{:S(2)}, u32[]{:S(2)}) collective-permute-start(f32[16,1152]{1,0:T(8,128)S(1)} %shard_map.76.rest_0_), channel_id=1, source_target_pairs={{0,192},{1,193},{2,194},{3,195},{4,196},{5,197},{6,198},{7,199},{8... | collective-permute-start | bytes 221192 | tf_op jit(solution)/shard_map/ppermute | solution.py:41
  69.9 1.2 %collective-permute-start.18 = (f32[16,1152]{1,0:T(8,128)S(1)}, f32[16,1152]{1,0:T(8,128)S(1)}, u32[]{:S(2)}, u32[]{:S(2)}) collective-permute-start(f32[16,1152]{1,0:T(8,128)S(1)} %shard_map.76.rest_0_), channel_id=1, source_target_pairs={{0,128},{1,129},{2,130},{3,131},{4,132},{5,133},{6,134},{7,135},{8... | collective-permute-start | bytes 221192 | tf_op jit(solution)/shard_map/ppermute | solution.py:41
  71.1 1.1 %collective-permute-done.16.rest_1_ = f32[16,1152]{1,0:T(8,128)S(1)} collective-permute-done((f32[16,1152]{1,0:T(8,128)S(1)}, f32[16,1152]{1,0:T(8,128)S(1)}, u32[]{:S(2)}, u32[]{:S(2)}) %collective-permute-start.16) | collective-permute-done | bytes 73760 | tf_op jit(solution)/shard_map/ppermute | solution.py:41
  72.2 0.3 collective-permute-done.17.rest_2_
  72.5 3.2 %collective-permute-done.18.rest_3_ = f32[16,1152]{1,0:T(8,128)S(1)} collective-permute-done((f32[16,1152]{1,0:T(8,128)S(1)}, f32[16,1152]{1,0:T(8,128)S(1)}, u32[]{:S(2)}, u32[]{:S(2)}) %collective-permute-start.18) | collective-permute-done | bytes 73760 | tf_op jit(solution)/shard_map/ppermute | solution.py:41
  75.7 1.3 %shard_map.77 = (f32[64,1024]{1,0:T(8,128)}, s32[8,8]{1,0:T(8,128)}) custom-call(s32[6]{0:T(128)S(1)} %stack.39.where, f32[16,1152]{1,0:T(8,128)S(1)} %shard_map.76.rest_0_, f32[16,1152]{1,0:T(8,128)S(1)} %collective-permute-done.16.rest_1_, f32[16,1152]{1,0:T(8,128)S(1)} %collective-permute-done.17.rest_2_, f32[16,1152]{1,0:T(8,128)S(1)} %collective-permute-done.18.rest_3_), custom_call_target="tpu_custom_call" | custom-call | tf_op jit(solution)/shard_map/pallas_call | solution.py:74
  (2 shorter events, 0.0 us)
Async XLA Ops:
  0.6 7.1 %collective-permute-start.1 = (bf16[1024,1024]{1,0:T(8,128)(2,1)}, bf16[1024,1024]{1,0:T(8,128)(2,1)S(1)}, u32[]{:S(2)}, u32[]{:S(2)}) collective-permute-start(bf16[1024,1024]{1,0:T(8,128)(2,1)} %pool_hbm.1), channel_id=1, source_target_pairs={{0,1},{1,0},{2,3},{3,2},{4,5},{5,4},{6,7},{7,6},{8,9},{9,8},{10,11... | collective-permute-start | bytes 6291464 | tf_op jit(solution)/shard_map/ppermute | solution.py:41
  1.5 3.6 %collective-permute-start = (s32[3,1,1024]{2,1,0:T(1,128)S(1)}, s32[3,1,1024]{2,1,0:T(1,128)S(1)}, u32[]{:S(2)}, u32[]{:S(2)}) collective-permute-start(s32[3,1,1024]{2,1,0:T(1,128)S(1)} %reshape.14.ints_ref), channel_id=1, source_target_pairs={{0,1},{1,0},{2,3},{3,2},{4,5},{5,4},{6,7},{7,6},{8,9},{9,8},{10,11... | collective-permute-start | bytes 36872 | tf_op jit(solution)/shard_map/ppermute | solution.py:41
  10.2 11.8 %collective-permute-start.2 = (bf16[2056,128]{1,0:T(8,128)(2,1)S(1)}, bf16[2056,128]{1,0:T(8,128)(2,1)S(1)}, u32[]{:S(2)}, u32[]{:S(2)}) collective-permute-start(bf16[2056,128]{1,0:T(8,128)(2,1)S(1)} %get-tuple-element.34), channel_id=1, source_target_pairs={{0,34},{1,143},{2,32},{3,133},{4,38},{5,131},{6,36},{7,137},{8,42}... | collective-permute-start | bytes 1579016 | tf_op jit(solution)/shard_map/ppermute | solution.py:41
  12.0 16.3 %collective-permute-start.3 = (bf16[2056,128]{1,0:T(8,128)(2,1)S(1)}, bf16[2056,128]{1,0:T(8,128)(2,1)S(1)}, u32[]{:S(2)}, u32[]{:S(2)}) collective-permute-start(bf16[2056,128]{1,0:T(8,128)(2,1)S(1)} %get-tuple-element.35), channel_id=1, source_target_pairs={{0,32},{1,129},{2,34},{3,131},{4,36},{5,133},{6,38},{7,135},{8,40}... | collective-permute-start | bytes 1579016 | tf_op jit(solution)/shard_map/ppermute | solution.py:41
  13.3 15.5 %collective-permute-start.4 = (bf16[2056,128]{1,0:T(8,128)(2,1)S(1)}, bf16[2056,128]{1,0:T(8,128)(2,1)S(1)}, u32[]{:S(2)}, u32[]{:S(2)}) collective-permute-start(bf16[2056,128]{1,0:T(8,128)(2,1)S(1)} %get-tuple-element.36), channel_id=1, source_target_pairs={{0,2},{1,15},{2,0},{3,5},{4,6},{5,3},{6,4},{7,9},{8,10},{9,7},{10,... | collective-permute-start | bytes 1579016 | tf_op jit(solution)/shard_map/ppermute | solution.py:41
  18.7 14.5 %collective-permute-start.5 = (bf16[2056,128]{1,0:T(8,128)(2,1)S(1)}, bf16[2056,128]{1,0:T(8,128)(2,1)S(1)}, u32[]{:S(2)}, u32[]{:S(2)}) collective-permute-start(bf16[2056,128]{1,0:T(8,128)(2,1)S(1)} %get-tuple-element.37), channel_id=1, source_target_pairs={{0,18},{1,79},{2,16},{3,69},{4,22},{5,67},{6,20},{7,73},{8,26},{9,... | collective-permute-start | bytes 1579016 | tf_op jit(solution)/shard_map/ppermute | solution.py:41
  19.6 17.3 %collective-permute-start.6 = (bf16[2056,128]{1,0:T(8,128)(2,1)S(1)}, bf16[2056,128]{1,0:T(8,128)(2,1)S(1)}, u32[]{:S(2)}, u32[]{:S(2)}) collective-permute-start(bf16[2056,128]{1,0:T(8,128)(2,1)S(1)} %get-tuple-element.40), channel_id=1, source_target_pairs={{0,48},{1,193},{2,50},{3,195},{4,52},{5,197},{6,54},{7,199},{8,56}... | collective-permute-start | bytes 1579016 | tf_op jit(solution)/shard_map/ppermute | solution.py:41
  22.0 15.9 %collective-permute-start.7 = (bf16[2056,128]{1,0:T(8,128)(2,1)S(1)}, bf16[2056,128]{1,0:T(8,128)(2,1)S(1)}, u32[]{:S(2)}, u32[]{:S(2)}) collective-permute-start(bf16[2056,128]{1,0:T(8,128)(2,1)S(1)} %get-tuple-element.41), channel_id=1, source_target_pairs={{0,50},{1,207},{2,48},{3,197},{4,54},{5,195},{6,52},{7,201},{8,58}... | collective-permute-start | bytes 1579016 | tf_op jit(solution)/shard_map/ppermute | solution.py:41
  28.3 10.5 %collective-permute-start.8 = (bf16[2056,128]{1,0:T(8,128)(2,1)S(1)}, bf16[2056,128]{1,0:T(8,128)(2,1)S(1)}, u32[]{:S(2)}, u32[]{:S(2)}) collective-permute-start(bf16[2056,128]{1,0:T(8,128)(2,1)S(1)} %get-tuple-element.42), channel_id=1, source_target_pairs={{0,16},{1,65},{2,18},{3,67},{4,20},{5,69},{6,22},{7,71},{8,24},{9,... | collective-permute-start | bytes 1579016 | tf_op jit(solution)/shard_map/ppermute | solution.py:41
  38.8 27.2 %copy-start = (f32[8,8,1024]{2,1,0:T(8,128)S(1)}, f32[8,8,1024]{2,1,0:T(8,128)}, u32[]{:S(2)}) copy-start(f32[8,8,1024]{2,1,0:T(8,128)} %param.9) | copy-start | bytes 786436
  39.7 8.1 %collective-permute-start.9 = (f32[520,128]{1,0:T(8,128)S(1)}, f32[520,128]{1,0:T(8,128)S(1)}, u32[]{:S(2)}, u32[]{:S(2)}) collective-permute-start(f32[520,128]{1,0:T(8,128)S(1)} %get-tuple-element.45), channel_id=1, source_target_pairs={{0,128},{1,33},{2,130},{3,35},{4,132},{5,37},{6,134},{7,39},{8,136... | collective-permute-start | bytes 798728 | tf_op jit(solution)/shard_map/ppermute | solution.py:41
  42.2 8.4 %collective-permute-start.10 = (f32[520,128]{1,0:T(8,128)S(1)}, f32[520,128]{1,0:T(8,128)S(1)}, u32[]{:S(2)}, u32[]{:S(2)}) collective-permute-start(f32[520,128]{1,0:T(8,128)S(1)} %get-tuple-element.46), channel_id=1, source_target_pairs={{0,64},{1,17},{2,66},{3,19},{4,68},{5,21},{6,70},{7,23},{8,72},{9,... | collective-permute-start | bytes 798728 | tf_op jit(solution)/shard_map/ppermute | solution.py:41
  42.9 7.7 %collective-permute-start.11 = (f32[520,128]{1,0:T(8,128)S(1)}, f32[520,128]{1,0:T(8,128)S(1)}, u32[]{:S(2)}, u32[]{:S(2)}) collective-permute-start(f32[520,128]{1,0:T(8,128)S(1)} %get-tuple-element.47), channel_id=1, source_target_pairs={{0,192},{1,49},{2,194},{3,51},{4,196},{5,53},{6,198},{7,55},{8,200... | collective-permute-start | bytes 798728 | tf_op jit(solution)/shard_map/ppermute | solution.py:41
  50.7 10.9 %collective-permute-start.12 = (f32[136,128]{1,0:T(8,128)S(1)}, f32[136,128]{1,0:T(8,128)S(1)}, u32[]{:S(2)}, u32[]{:S(2)}) collective-permute-start(f32[136,128]{1,0:T(8,128)S(1)} %get-tuple-element.49), channel_id=1, source_target_pairs={{0,8},{1,9},{2,10},{3,11},{4,12},{5,13},{6,14},{7,15},{8,0},{9,1},... | collective-permute-start | bytes 208904 | tf_op jit(solution)/shard_map/ppermute | solution.py:41
  57.4 7.2 %collective-permute-start.13 = (f32[136,128]{1,0:T(8,128)S(1)}, f32[136,128]{1,0:T(8,128)S(1)}, u32[]{:S(2)}, u32[]{:S(2)}) collective-permute-start(f32[136,128]{1,0:T(8,128)S(1)} %get-tuple-element.50), channel_id=1, source_target_pairs={{0,4},{1,5},{2,6},{3,7},{4,8},{5,9},{6,10},{7,11},{8,12},{9,13},{1... | collective-permute-start | bytes 208904 | tf_op jit(solution)/shard_map/ppermute | solution.py:41
  58.9 5.8 %collective-permute-start.14 = (f32[136,128]{1,0:T(8,128)S(1)}, f32[136,128]{1,0:T(8,128)S(1)}, u32[]{:S(2)}, u32[]{:S(2)}) collective-permute-start(f32[136,128]{1,0:T(8,128)S(1)} %get-tuple-element.51), channel_id=1, source_target_pairs={{0,12},{1,13},{2,14},{3,15},{4,0},{5,1},{6,2},{7,3},{8,4},{9,5},{1... | collective-permute-start | bytes 208904 | tf_op jit(solution)/shard_map/ppermute | solution.py:41
  64.6 1.3 %collective-permute-start.15 = (f32[64,128]{1,0:T(8,128)S(1)}, f32[64,128]{1,0:T(8,128)S(1)}, u32[]{:S(2)}, u32[]{:S(2)}) collective-permute-start(f32[64,128]{1,0:T(8,128)S(1)} %get-tuple-element.53), channel_id=1, source_target_pairs={{0,1},{1,0},{2,3},{3,2},{4,5},{5,4},{6,7},{7,6},{8,9},{9,8},{10,11... | collective-permute-start | bytes 98312 | tf_op jit(solution)/shard_map/ppermute | solution.py:41
  66.6 5.6 %collective-permute-start.16 = (f32[16,1152]{1,0:T(8,128)S(1)}, f32[16,1152]{1,0:T(8,128)S(1)}, u32[]{:S(2)}, u32[]{:S(2)}) collective-permute-start(f32[16,1152]{1,0:T(8,128)S(1)} %shard_map.76.rest_0_), channel_id=1, source_target_pairs={{0,64},{1,65},{2,66},{3,67},{4,68},{5,69},{6,70},{7,71},{8,72},{9,... | collective-permute-start | bytes 221192 | tf_op jit(solution)/shard_map/ppermute | solution.py:41
  68.1 4.4 %collective-permute-start.17 = (f32[16,1152]{1,0:T(8,128)S(1)}, f32[16,1152]{1,0:T(8,128)S(1)}, u32[]{:S(2)}, u32[]{:S(2)}) collective-permute-start(f32[16,1152]{1,0:T(8,128)S(1)} %shard_map.76.rest_0_), channel_id=1, source_target_pairs={{0,192},{1,193},{2,194},{3,195},{4,196},{5,197},{6,198},{7,199},{8... | collective-permute-start | bytes 221192 | tf_op jit(solution)/shard_map/ppermute | solution.py:41
  69.9 5.9 %collective-permute-start.18 = (f32[16,1152]{1,0:T(8,128)S(1)}, f32[16,1152]{1,0:T(8,128)S(1)}, u32[]{:S(2)}, u32[]{:S(2)}) collective-permute-start(f32[16,1152]{1,0:T(8,128)S(1)} %shard_map.76.rest_0_), channel_id=1, source_target_pairs={{0,128},{1,129},{2,130},{3,131},{4,132},{5,133},{6,134},{7,135},{8... | collective-permute-start | bytes 221192 | tf_op jit(solution)/shard_map/ppermute | solution.py:41

commit v2 on v1

--- a/solution.py
+++ b/solution.py
@@ -25,7 +25,7 @@
 FIRST = 3
 CROSS = [0, 2, 1, 3]
 DEEP = [0, 2, 1, 3]
-TURNS = [0, 1, 3, 2]
+TURNS = [0, 2, 1, 3]
 EARLY = 4
 
 
@@ -136,9 +136,7 @@
 
 
 def pool_kernel(most, owned, kinds, where, ints_ref, pool_hbm, source_ref, label_ref, pool, sem):
-    width = pool.shape[1]
-    columns = pl.ds(pl.multiple_of(where[4] * width, width), width)
-    copy = pltpu.make_async_copy(pool_hbm.at[:, columns], pool, sem)
+    copy = pltpu.make_async_copy(pool_hbm, pool, sem)
     copy.start()
     source_ref[...], label_ref[...] = lines_of(where, most, owned, kinds, ints_ref)
     copy.wait()
@@ -146,7 +144,7 @@
 
 def fill_kernel(chunks, where, own_source, own_label, came_source, came_label, own_pool, came_pool, *rest):
     outs, select = rest[:-1], rest[-1]
-    rows, width = own_pool.shape
+    rows, width = own_pool.shape[0], own_pool.shape[1] // NC
     blocks = width // LANES
     most = own_source.shape[1]
     spots = own_source.shape[0] // CHUNKS
@@ -166,7 +164,7 @@
         outs[i][blocks * NC * chunk :, :] = tile.astype(jnp.bfloat16)
     columns = pl.ds(pl.multiple_of(where[4] * width, width), width)
     for k in range(NC):
-        pool = came_pool[:, columns] if k else own_pool[...]
+        pool = (came_pool if k else own_pool)[:, columns]
         for g in range(0, len(chunks), 2):
             some = min(2, len(chunks) - g)
             got = dot(select[k, g * chunk : (g + some) * chunk, :], pool).astype(jnp.bfloat16)
@@ -248,11 +246,9 @@
     mine_ref[part:, :] = total[NC * part :]
 
 
-def finish_kernel(kinds, where, old_ref, mine_ref, came_ref, out, sums):
+def finish_kernel(kinds, where, old_ref, mine_ref, came_ref, out):
     half, width = came_ref.shape[0], old_ref.shape[1]
     core = where[4]
-    sums[pl.ds(pl.multiple_of(core * half, half), half), :] = mine_ref[:half, :]
-    sums[pl.ds(pl.multiple_of((1 - core) * half, half), half), :] = came_ref[...]
     blocks = width // LANES
     part = 2 * half // blocks
     lane = iota((part, LANES), 1)
@@ -262,7 +258,9 @@
     rows = pl.ds(pl.multiple_of(where[5] * part, part), part)
     for k in range(blocks):
         at = slice(k * LANES, (k + 1) * LANES)
-        out[:, at] = (sums[k * part : (k + 1) * part, :] + old_ref[rows, at]) / divisor
+        rest = slice(k % (blocks // NC) * part, (k % (blocks // NC) + 1) * part)
+        total = jnp.where(core == k // (blocks // NC), mine_ref[rest, :], came_ref[rest, :])
+        out[:, at] = (total + old_ref[rows, at]) / divisor
     count = jnp.where(lane == lax.rem(iota((part, LANES), 0), kinds), count, 0.0)
     line = iota((part, LANES), 0)
     tile = jnp.zeros((part, LANES), jnp.float32)
@@ -306,7 +304,7 @@
     own_lines = call(functools.partial(lines_kernel, most, owned, kinds), lines, [SMEM, VMEM], [where, ints])
     *came_lines, own_pool = call(
         functools.partial(pool_kernel, most, owned, kinds),
-        [*lines, shape(rows, half, dtype=jnp.bfloat16)],
+        [*lines, shape(rows, width, dtype=jnp.bfloat16)],
         [SMEM, VMEM, HBM],
         [where, came_ints, pltpu.with_memory_space_constraint(pool_rows, HBM)],
         [DMA],
@@ -346,9 +344,10 @@
         shape(part, width + LANES),
         [SMEM, VMEM, VMEM, VMEM],
         [where, old_centroids.reshape(block * kinds, width), mine, permute(other, other_core)],
-        [VMEM((NC * blocks * part, LANES), jnp.float32)],
-    )
-    quarters = [fresh] + [permute(fresh, lambda y, x, z, c, t=t: (y + t, x, z, c)) for t in TURNS[1:]]
+    )
+    quarters = [fresh]
+    for t in TURNS[1:]:
+        quarters.append(permute(fresh, lambda y, x, z, c, t=t: (y + t, x, z, c)))
     centroids, counts = call(
         place_kernel,
         [shape(block * kinds, width), shape(block, kinds, dtype=jnp.int32)],

time: 78.4 us -> 77.3 us (0.986)
  the two profiles are of different devices: /device:TPU:36 before, /device:TPU:1 now
where the time goes in v2:
time: 77.3 us; the launch traced here: 77.1 us
  starting transfers between devices  39.4 us (51%)
  waiting for transfers between devices  22.7 us (29%)
  Pallas kernels  13.4 us (17%)
    ppermute x19, starting transfers between devices, permute(): return lax.ppermute(value, AXES, pairs)  39.4 us
    ppermute x19, waiting for transfers between devices, permute(): return lax.ppermute(value, AXES, pairs)  22.7 us
    pallas_call x10, Pallas kernels, call(): pl.pallas_call(kernel, out_shape=outs, in_specs=[pl.BlockSpec(memory_spac...  13.4 us
  transfers between devices with their start and end apart: 19, of which 15 were waited for; matrix products, arithmetic and copies ran while one was open for 1% of the time, Pallas kernels for 10%

profile of v2, /device:TPU:1, one launch (start us, length us, event | category | flops | bytes accessed | tf_op | source)
XLA Modules:
  0.0 77.1 jit_solution(4787585528453753665)
XLA Ops:
  0.6 3.3 %collective-permute-start.1 = (bf16[1024,1024]{1,0:T(8,128)(2,1)}, bf16[1024,1024]{1,0:T(8,128)(2,1)S(1)}, u32[]{:S(2)}, u32[]{:S(2)}) collective-permute-start(bf16[1024,1024]{1,0:T(8,128)(2,1)} %pool_hbm.1), channel_id=1, source_target_pairs={{0,1},{1,0},{2,3},{3,2},{4,5},{5,4},{6,7},{7,6},{8,9},{9,8},{10,11... | collective-permute-start | bytes 6291464 | tf_op jit(solution)/shard_map/ppermute | solution.py:41
  3.9 0.7 pad_add_fusion
  4.7 0.1 collective-permute-start
  4.8 0.1 stack.39.where
  4.9 1.5 %shard_map.68 = (f32[256,8]{1,0:T(8,128)S(1)}, f32[16,128]{1,0:T(8,128)S(1)}) custom-call(s32[6]{0:T(128)S(1)} %stack.39.where, s32[3,1,1024]{2,1,0:T(1,128)S(1)} %reshape.14.ints_ref), custom_call_target="tpu_custom_call" | custom-call | tf_op jit(solution)/shard_map/pallas_call | solution.py:74
  6.4 1.6 %collective-permute-done.ints_ref = s32[3,1,1024]{2,1,0:T(1,128)S(1)} collective-permute-done((s32[3,1,1024]{2,1,0:T(1,128)S(1)}, s32[3,1,1024]{2,1,0:T(1,128)S(1)}, u32[]{:S(2)}, u32[]{:S(2)}) %collective-permute-start) | collective-permute-done | bytes 12320 | tf_op jit(solution)/shard_map/ppermute | solution.py:41
  7.9 2.1 %shard_map.69 = (f32[256,8]{1,0:T(8,128)S(1)}, f32[16,128]{1,0:T(8,128)S(1)}, bf16[1024,1024]{1,0:T(8,128)(2,1)S(1)}) custom-call(s32[6]{0:T(128)S(1)} %stack.39.where, s32[3,1,1024]{2,1,0:T(1,128)S(1)} %collective-permute-done.ints_ref, bf16[1024,1024]{1,0:T(8,128)(2,1)} %pool_hbm.1), custom_call_target="tpu_custom_call" | custom-call | tf_op jit(solution)/shard_map/pallas_call | solution.py:74
  10.1 0.0 collective-permute-done.1.came_pool
  10.1 2.4 %shard_map.70 = (bf16[2056,128]{1,0:T(8,128)(2,1)S(1)}, bf16[2056,128]{1,0:T(8,128)(2,1)S(1)}, bf16[2056,128]{1,0:T(8,128)(2,1)S(1)}) custom-call(s32[6]{0:T(128)S(1)} %stack.39.where, f32[256,8]{1,0:T(8,128)S(1)} %get-tuple-element.29.own_source, f32[16,128]{1,0:T(8,128)S(1)} %get-tuple-element.30.own_label, f32[256,8]{1,0:T(8,128)S(1)} %get-tuple-element.31.came_source, ...), custom_call_target="tpu_custom_call" | custom-call | tf_op jit(solution)/shard_map/pallas_call | solution.py:74
  12.5 6.6 %collective-permute-start.2 = (bf16[2056,128]{1,0:T(8,128)(2,1)S(1)}, bf16[2056,128]{1,0:T(8,128)(2,1)S(1)}, u32[]{:S(2)}, u32[]{:S(2)}) collective-permute-start(bf16[2056,128]{1,0:T(8,128)(2,1)S(1)} %get-tuple-element.34), channel_id=1, source_target_pairs={{0,34},{1,143},{2,32},{3,133},{4,38},{5,131},{6,36},{7,137},{8,42}... | collective-permute-start | bytes 1579016 | tf_op jit(solution)/shard_map/ppermute | solution.py:41
  19.1 0.1 collective-permute-start.3
  19.1 0.3 collective-permute-start.4
  19.5 3.5 %shard_map.71 = (bf16[2056,128]{1,0:T(8,128)(2,1)S(1)}, bf16[2056,128]{1,0:T(8,128)(2,1)S(1)}, bf16[2056,128]{1,0:T(8,128)(2,1)S(1)}, bf16[2056,128]{1,0:T(8,128)(2,1)S(1)}, bf16[2056,128]{1,0:T(8,128)(2,1)S(1)}) custom-call(s32[6]{0:T(128)S(1)} %stack.39.where, f32[256,8]{1,0:T(8,128)S(1)} %get-tuple-element.29.own_source, ...), custom_call_target="tpu_custom_call" | custom-call | tf_op jit(solution)/shard_map/pallas_call | solution.py:74
  22.9 3.4 %collective-permute-start.5 = (bf16[2056,128]{1,0:T(8,128)(2,1)S(1)}, bf16[2056,128]{1,0:T(8,128)(2,1)S(1)}, u32[]{:S(2)}, u32[]{:S(2)}) collective-permute-start(bf16[2056,128]{1,0:T(8,128)(2,1)S(1)} %get-tuple-element.37), channel_id=1, source_target_pairs={{0,18},{1,79},{2,16},{3,69},{4,22},{5,67},{6,20},{7,73},{8,26},{9,... | collective-permute-start | bytes 1579016 | tf_op jit(solution)/shard_map/ppermute | solution.py:41
  26.4 1.4 %collective-permute-start.6 = (bf16[2056,128]{1,0:T(8,128)(2,1)S(1)}, bf16[2056,128]{1,0:T(8,128)(2,1)S(1)}, u32[]{:S(2)}, u32[]{:S(2)}) collective-permute-start(bf16[2056,128]{1,0:T(8,128)(2,1)S(1)} %get-tuple-element.40), channel_id=1, source_target_pairs={{0,48},{1,193},{2,50},{3,195},{4,52},{5,197},{6,54},{7,199},{8,56}... | collective-permute-start | bytes 1579016 | tf_op jit(solution)/shard_map/ppermute | solution.py:41
  27.8 0.0 collective-permute-done.2.rest_0_
  27.8 2.9 %collective-permute-start.7 = (bf16[2056,128]{1,0:T(8,128)(2,1)S(1)}, bf16[2056,128]{1,0:T(8,128)(2,1)S(1)}, u32[]{:S(2)}, u32[]{:S(2)}) collective-permute-start(bf16[2056,128]{1,0:T(8,128)(2,1)S(1)} %get-tuple-element.41), channel_id=1, source_target_pairs={{0,50},{1,207},{2,48},{3,197},{4,54},{5,195},{6,52},{7,201},{8,58}... | collective-permute-start | bytes 1579016 | tf_op jit(solution)/shard_map/ppermute | solution.py:41
  30.7 0.9 %collective-permute-done.3.rest_1_ = bf16[2056,128]{1,0:T(8,128)(2,1)S(1)} collective-permute-done((bf16[2056,128]{1,0:T(8,128)(2,1)S(1)}, bf16[2056,128]{1,0:T(8,128)(2,1)S(1)}, u32[]{:S(2)}, u32[]{:S(2)}) %collective-permute-start.3) | collective-permute-done | bytes 526368 | tf_op jit(solution)/shard_map/ppermute | solution.py:41
  31.6 0.4 collective-permute-start.8
  32.0 0.0 collective-permute-done.4.rest_2_
  32.0 5.0 %collective-permute-done.5.rest_3_ = bf16[2056,128]{1,0:T(8,128)(2,1)S(1)} collective-permute-done((bf16[2056,128]{1,0:T(8,128)(2,1)S(1)}, bf16[2056,128]{1,0:T(8,128)(2,1)S(1)}, u32[]{:S(2)}, u32[]{:S(2)}) %collective-permute-start.5) | collective-permute-done | bytes 526368 | tf_op jit(solution)/shard_map/ppermute | solution.py:41
  37.0 1.0 %shard_map.72 = (f32[512,512]{1,0:T(8,128)S(1)}, f32[2,8,256]{2,1,0:T(8,128)S(1)}) custom-call(bf16[2056,128]{1,0:T(8,128)(2,1)S(1)} %collective-permute-done.2.rest_0_, bf16[2056,128]{1,0:T(8,128)(2,1)S(1)} %collective-permute-done.3.rest_1_, bf16[2056,128]{1,0:T(8,128)(2,1)S(1)} %collective-permute-done.4.rest_2_, ...), custom_call_target="tpu_custom_call" | custom-call | tf_op jit(solution)/shard_map/pallas_call | solution.py:74
  38.0 2.2 %collective-permute-done.6.rest_0_ = bf16[2056,128]{1,0:T(8,128)(2,1)S(1)} collective-permute-done((bf16[2056,128]{1,0:T(8,128)(2,1)S(1)}, bf16[2056,128]{1,0:T(8,128)(2,1)S(1)}, u32[]{:S(2)}, u32[]{:S(2)}) %collective-permute-start.6) | collective-permute-done | bytes 526368 | tf_op jit(solution)/shard_map/ppermute | solution.py:41
  40.2 2.0 %collective-permute-done.7.rest_1_ = bf16[2056,128]{1,0:T(8,128)(2,1)S(1)} collective-permute-done((bf16[2056,128]{1,0:T(8,128)(2,1)S(1)}, bf16[2056,128]{1,0:T(8,128)(2,1)S(1)}, u32[]{:S(2)}, u32[]{:S(2)}) %collective-permute-start.7) | collective-permute-done | bytes 526368 | tf_op jit(solution)/shard_map/ppermute | solution.py:41
  42.2 0.4 collective-permute-done.8.rest_2_
  42.6 0.0 copy-start
  42.6 0.9 %shard_map.73 = (f32[520,128]{1,0:T(8,128)S(1)}, f32[520,128]{1,0:T(8,128)S(1)}, f32[520,128]{1,0:T(8,128)S(1)}, f32[520,128]{1,0:T(8,128)S(1)}) custom-call(f32[512,512]{1,0:T(8,128)S(1)} %get-tuple-element.38.sum_ref, f32[2,8,256]{2,1,0:T(8,128)S(1)} %get-tuple-element.39.tally_ref, bf16[2056,128]{1,0:T(8,128)(2,1)S(1)} %collective-permute-done.6.rest_0_, ...), custom_call_target="tpu_custom_call" | custom-call | tf_op jit(solution)/shard_map/pallas_call | solution.py:74
  43.5 2.8 %collective-permute-start.9 = (f32[520,128]{1,0:T(8,128)S(1)}, f32[520,128]{1,0:T(8,128)S(1)}, u32[]{:S(2)}, u32[]{:S(2)}) collective-permute-start(f32[520,128]{1,0:T(8,128)S(1)} %get-tuple-element.45), channel_id=1, source_target_pairs={{0,128},{1,33},{2,130},{3,35},{4,132},{5,37},{6,134},{7,39},{8,136... | collective-permute-start | bytes 798728 | tf_op jit(solution)/shard_map/ppermute | solution.py:41
  46.4 0.3 collective-permute-start.10
  46.7 2.4 %collective-permute-start.11 = (f32[520,128]{1,0:T(8,128)S(1)}, f32[520,128]{1,0:T(8,128)S(1)}, u32[]{:S(2)}, u32[]{:S(2)}) collective-permute-start(f32[520,128]{1,0:T(8,128)S(1)} %get-tuple-element.47), channel_id=1, source_target_pairs={{0,192},{1,49},{2,194},{3,51},{4,196},{5,53},{6,198},{7,55},{8,200... | collective-permute-start | bytes 798728 | tf_op jit(solution)/shard_map/ppermute | solution.py:41
  49.0 1.4 %collective-permute-done.9.rest_1_ = f32[520,128]{1,0:T(8,128)S(1)} collective-permute-done((f32[520,128]{1,0:T(8,128)S(1)}, f32[520,128]{1,0:T(8,128)S(1)}, u32[]{:S(2)}, u32[]{:S(2)}) %collective-permute-start.9) | collective-permute-done | bytes 266272 | tf_op jit(solution)/shard_map/ppermute | solution.py:41
  50.4 2.8 %collective-permute-done.10.rest_2_ = f32[520,128]{1,0:T(8,128)S(1)} collective-permute-done((f32[520,128]{1,0:T(8,128)S(1)}, f32[520,128]{1,0:T(8,128)S(1)}, u32[]{:S(2)}, u32[]{:S(2)}) %collective-permute-start.10) | collective-permute-done | bytes 266272 | tf_op jit(solution)/shard_map/ppermute | solution.py:41
  53.2 0.1 collective-permute-done.11.rest_3_
  53.3 0.1 shard_map.74
  53.4 4.9 %collective-permute-start.12 = (f32[136,128]{1,0:T(8,128)S(1)}, f32[136,128]{1,0:T(8,128)S(1)}, u32[]{:S(2)}, u32[]{:S(2)}) collective-permute-start(f32[136,128]{1,0:T(8,128)S(1)} %get-tuple-element.49), channel_id=1, source_target_pairs={{0,8},{1,9},{2,10},{3,11},{4,12},{5,13},{6,14},{7,15},{8,0},{9,1},... | collective-permute-start | bytes 208904 | tf_op jit(solution)/shard_map/ppermute | solution.py:41
  58.3 0.3 collective-permute-start.13
  58.6 3.3 %collective-permute-start.14 = (f32[136,128]{1,0:T(8,128)S(1)}, f32[136,128]{1,0:T(8,128)S(1)}, u32[]{:S(2)}, u32[]{:S(2)}) collective-permute-start(f32[136,128]{1,0:T(8,128)S(1)} %get-tuple-element.51), channel_id=1, source_target_pairs={{0,12},{1,13},{2,14},{3,15},{4,0},{5,1},{6,2},{7,3},{8,4},{9,5},{1... | collective-permute-start | bytes 208904 | tf_op jit(solution)/shard_map/ppermute | solution.py:41
  61.9 0.0 collective-permute-done.12.rest_1_
  61.9 1.7 %collective-permute-done.13.rest_2_ = f32[136,128]{1,0:T(8,128)S(1)} collective-permute-done((f32[136,128]{1,0:T(8,128)S(1)}, f32[136,128]{1,0:T(8,128)S(1)}, u32[]{:S(2)}, u32[]{:S(2)}) %collective-permute-start.13) | collective-permute-done | bytes 69664 | tf_op jit(solution)/shard_map/ppermute | solution.py:41
  63.6 1.4 %collective-permute-done.14.rest_3_ = f32[136,128]{1,0:T(8,128)S(1)} collective-permute-done((f32[136,128]{1,0:T(8,128)S(1)}, f32[136,128]{1,0:T(8,128)S(1)}, u32[]{:S(2)}, u32[]{:S(2)}) %collective-permute-start.14) | collective-permute-done | bytes 69664 | tf_op jit(solution)/shard_map/ppermute | solution.py:41
  65.0 2.4 %collective-permute-start.15 = (f32[64,128]{1,0:T(8,128)S(1)}, f32[64,128]{1,0:T(8,128)S(1)}, u32[]{:S(2)}, u32[]{:S(2)}) collective-permute-start(f32[64,128]{1,0:T(8,128)S(1)} %get-tuple-element.53), channel_id=1, source_target_pairs={{0,1},{1,0},{2,3},{3,2},{4,5},{5,4},{6,7},{7,6},{8,9},{9,8},{10,11... | collective-permute-start | bytes 98312 | tf_op jit(solution)/shard_map/ppermute | solution.py:41
  67.4 0.9 %collective-permute-done.15.came_ref = f32[64,128]{1,0:T(8,128)S(1)} collective-permute-done((f32[64,128]{1,0:T(8,128)S(1)}, f32[64,128]{1,0:T(8,128)S(1)}, u32[]{:S(2)}, u32[]{:S(2)}) %collective-permute-start.15) | collective-permute-done | bytes 32800 | tf_op jit(solution)/shard_map/ppermute | solution.py:41
  68.2 0.0 copy-done
  68.3 0.6 shard_map.76.rest_0_
  68.9 1.9 %collective-permute-start.16 = (f32[16,1152]{1,0:T(8,128)S(1)}, f32[16,1152]{1,0:T(8,128)S(1)}, u32[]{:S(2)}, u32[]{:S(2)}) collective-permute-start(f32[16,1152]{1,0:T(8,128)S(1)} %shard_map.76.rest_0_), channel_id=1, source_target_pairs={{0,128},{1,129},{2,130},{3,131},{4,132},{5,133},{6,134},{7,135},{8... | collective-permute-start | bytes 221192 | tf_op jit(solution)/shard_map/ppermute | solution.py:41
  70.8 1.4 %collective-permute-start.17 = (f32[16,1152]{1,0:T(8,128)S(1)}, f32[16,1152]{1,0:T(8,128)S(1)}, u32[]{:S(2)}, u32[]{:S(2)}) collective-permute-start(f32[16,1152]{1,0:T(8,128)S(1)} %shard_map.76.rest_0_), channel_id=1, source_target_pairs={{0,64},{1,65},{2,66},{3,67},{4,68},{5,69},{6,70},{7,71},{8,72},{9,... | collective-permute-start | bytes 221192 | tf_op jit(solution)/shard_map/ppermute | solution.py:41
  72.2 1.2 %collective-permute-start.18 = (f32[16,1152]{1,0:T(8,128)S(1)}, f32[16,1152]{1,0:T(8,128)S(1)}, u32[]{:S(2)}, u32[]{:S(2)}) collective-permute-start(f32[16,1152]{1,0:T(8,128)S(1)} %shard_map.76.rest_0_), channel_id=1, source_target_pairs={{0,192},{1,193},{2,194},{3,195},{4,196},{5,197},{6,198},{7,199},{8... | collective-permute-start | bytes 221192 | tf_op jit(solution)/shard_map/ppermute | solution.py:41
  73.4 0.2 collective-permute-done.16.rest_1_
  73.7 1.6 %collective-permute-done.17.rest_2_ = f32[16,1152]{1,0:T(8,128)S(1)} collective-permute-done((f32[16,1152]{1,0:T(8,128)S(1)}, f32[16,1152]{1,0:T(8,128)S(1)}, u32[]{:S(2)}, u32[]{:S(2)}) %collective-permute-start.17) | collective-permute-done | bytes 73760 | tf_op jit(solution)/shard_map/ppermute | solution.py:41
  75.3 0.6 collective-permute-done.18.rest_3_
  75.8 1.3 %shard_map.77 = (f32[64,1024]{1,0:T(8,128)}, s32[8,8]{1,0:T(8,128)}) custom-call(s32[6]{0:T(128)S(1)} %stack.39.where, f32[16,1152]{1,0:T(8,128)S(1)} %shard_map.76.rest_0_, f32[16,1152]{1,0:T(8,128)S(1)} %collective-permute-done.16.rest_1_, f32[16,1152]{1,0:T(8,128)S(1)} %collective-permute-done.17.rest_2_, f32[16,1152]{1,0:T(8,128)S(1)} %collective-permute-done.18.rest_3_), custom_call_target="tpu_custom_call" | custom-call | tf_op jit(solution)/shard_map/pallas_call | solution.py:74
  (2 shorter events, 0.0 us)
Async XLA Ops:
  0.6 9.5 %collective-permute-start.1 = (bf16[1024,1024]{1,0:T(8,128)(2,1)}, bf16[1024,1024]{1,0:T(8,128)(2,1)S(1)}, u32[]{:S(2)}, u32[]{:S(2)}) collective-permute-start(bf16[1024,1024]{1,0:T(8,128)(2,1)} %pool_hbm.1), channel_id=1, source_target_pairs={{0,1},{1,0},{2,3},{3,2},{4,5},{5,4},{6,7},{7,6},{8,9},{9,8},{10,11... | collective-permute-start | bytes 6291464 | tf_op jit(solution)/shard_map/ppermute | solution.py:41
  4.7 3.3 %collective-permute-start = (s32[3,1,1024]{2,1,0:T(1,128)S(1)}, s32[3,1,1024]{2,1,0:T(1,128)S(1)}, u32[]{:S(2)}, u32[]{:S(2)}) collective-permute-start(s32[3,1,1024]{2,1,0:T(1,128)S(1)} %reshape.14.ints_ref), channel_id=1, source_target_pairs={{0,1},{1,0},{2,3},{3,2},{4,5},{5,4},{6,7},{7,6},{8,9},{9,8},{10,11... | collective-permute-start | bytes 36872 | tf_op jit(solution)/shard_map/ppermute | solution.py:41
  12.5 15.3 %collective-permute-start.2 = (bf16[2056,128]{1,0:T(8,128)(2,1)S(1)}, bf16[2056,128]{1,0:T(8,128)(2,1)S(1)}, u32[]{:S(2)}, u32[]{:S(2)}) collective-permute-start(bf16[2056,128]{1,0:T(8,128)(2,1)S(1)} %get-tuple-element.34), channel_id=1, source_target_pairs={{0,34},{1,143},{2,32},{3,133},{4,38},{5,131},{6,36},{7,137},{8,42}... | collective-permute-start | bytes 1579016 | tf_op jit(solution)/shard_map/ppermute | solution.py:41
  19.1 12.5 %collective-permute-start.3 = (bf16[2056,128]{1,0:T(8,128)(2,1)S(1)}, bf16[2056,128]{1,0:T(8,128)(2,1)S(1)}, u32[]{:S(2)}, u32[]{:S(2)}) collective-permute-start(bf16[2056,128]{1,0:T(8,128)(2,1)S(1)} %get-tuple-element.35), channel_id=1, source_target_pairs={{0,32},{1,129},{2,34},{3,131},{4,36},{5,133},{6,38},{7,135},{8,40}... | collective-permute-start | bytes 1579016 | tf_op jit(solution)/shard_map/ppermute | solution.py:41
  19.1 12.9 %collective-permute-start.4 = (bf16[2056,128]{1,0:T(8,128)(2,1)S(1)}, bf16[2056,128]{1,0:T(8,128)(2,1)S(1)}, u32[]{:S(2)}, u32[]{:S(2)}) collective-permute-start(bf16[2056,128]{1,0:T(8,128)(2,1)S(1)} %get-tuple-element.36), channel_id=1, source_target_pairs={{0,2},{1,15},{2,0},{3,5},{4,6},{5,3},{6,4},{7,9},{8,10},{9,7},{10,... | collective-permute-start | bytes 1579016 | tf_op jit(solution)/shard_map/ppermute | solution.py:41
  22.9 14.1 %collective-permute-start.5 = (bf16[2056,128]{1,0:T(8,128)(2,1)S(1)}, bf16[2056,128]{1,0:T(8,128)(2,1)S(1)}, u32[]{:S(2)}, u32[]{:S(2)}) collective-permute-start(bf16[2056,128]{1,0:T(8,128)(2,1)S(1)} %get-tuple-element.37), channel_id=1, source_target_pairs={{0,18},{1,79},{2,16},{3,69},{4,22},{5,67},{6,20},{7,73},{8,26},{9,... | collective-permute-start | bytes 1579016 | tf_op jit(solution)/shard_map/ppermute | solution.py:41
  26.4 13.9 %collective-permute-start.6 = (bf16[2056,128]{1,0:T(8,128)(2,1)S(1)}, bf16[2056,128]{1,0:T(8,128)(2,1)S(1)}, u32[]{:S(2)}, u32[]{:S(2)}) collective-permute-start(bf16[2056,128]{1,0:T(8,128)(2,1)S(1)} %get-tuple-element.40), channel_id=1, source_target_pairs={{0,48},{1,193},{2,50},{3,195},{4,52},{5,197},{6,54},{7,199},{8,56}... | collective-permute-start | bytes 1579016 | tf_op jit(solution)/shard_map/ppermute | solution.py:41
  27.8 14.5 %collective-permute-start.7 = (bf16[2056,128]{1,0:T(8,128)(2,1)S(1)}, bf16[2056,128]{1,0:T(8,128)(2,1)S(1)}, u32[]{:S(2)}, u32[]{:S(2)}) collective-permute-start(bf16[2056,128]{1,0:T(8,128)(2,1)S(1)} %get-tuple-element.41), channel_id=1, source_target_pairs={{0,50},{1,207},{2,48},{3,197},{4,54},{5,195},{6,52},{7,201},{8,58}... | collective-permute-start | bytes 1579016 | tf_op jit(solution)/shard_map/ppermute | solution.py:41
  31.6 11.0 %collective-permute-start.8 = (bf16[2056,128]{1,0:T(8,128)(2,1)S(1)}, bf16[2056,128]{1,0:T(8,128)(2,1)S(1)}, u32[]{:S(2)}, u32[]{:S(2)}) collective-permute-start(bf16[2056,128]{1,0:T(8,128)(2,1)S(1)} %get-tuple-element.42), channel_id=1, source_target_pairs={{0,16},{1,65},{2,18},{3,67},{4,20},{5,69},{6,22},{7,71},{8,24},{9,... | collective-permute-start | bytes 1579016 | tf_op jit(solution)/shard_map/ppermute | solution.py:41
  42.6 25.7 %copy-start = (f32[8,8,1024]{2,1,0:T(8,128)S(1)}, f32[8,8,1024]{2,1,0:T(8,128)}, u32[]{:S(2)}) copy-start(f32[8,8,1024]{2,1,0:T(8,128)} %param.9) | copy-start | bytes 786436
  43.5 6.9 %collective-permute-start.9 = (f32[520,128]{1,0:T(8,128)S(1)}, f32[520,128]{1,0:T(8,128)S(1)}, u32[]{:S(2)}, u32[]{:S(2)}) collective-permute-start(f32[520,128]{1,0:T(8,128)S(1)} %get-tuple-element.45), channel_id=1, source_target_pairs={{0,128},{1,33},{2,130},{3,35},{4,132},{5,37},{6,134},{7,39},{8,136... | collective-permute-start | bytes 798728 | tf_op jit(solution)/shard_map/ppermute | solution.py:41
  46.4 6.9 %collective-permute-start.10 = (f32[520,128]{1,0:T(8,128)S(1)}, f32[520,128]{1,0:T(8,128)S(1)}, u32[]{:S(2)}, u32[]{:S(2)}) collective-permute-start(f32[520,128]{1,0:T(8,128)S(1)} %get-tuple-element.46), channel_id=1, source_target_pairs={{0,64},{1,17},{2,66},{3,19},{4,68},{5,21},{6,70},{7,23},{8,72},{9,... | collective-permute-start | bytes 798728 | tf_op jit(solution)/shard_map/ppermute | solution.py:41
  46.7 6.7 %collective-permute-start.11 = (f32[520,128]{1,0:T(8,128)S(1)}, f32[520,128]{1,0:T(8,128)S(1)}, u32[]{:S(2)}, u32[]{:S(2)}) collective-permute-start(f32[520,128]{1,0:T(8,128)S(1)} %get-tuple-element.47), channel_id=1, source_target_pairs={{0,192},{1,49},{2,194},{3,51},{4,196},{5,53},{6,198},{7,55},{8,200... | collective-permute-start | bytes 798728 | tf_op jit(solution)/shard_map/ppermute | solution.py:41
  53.4 8.5 %collective-permute-start.12 = (f32[136,128]{1,0:T(8,128)S(1)}, f32[136,128]{1,0:T(8,128)S(1)}, u32[]{:S(2)}, u32[]{:S(2)}) collective-permute-start(f32[136,128]{1,0:T(8,128)S(1)} %get-tuple-element.49), channel_id=1, source_target_pairs={{0,8},{1,9},{2,10},{3,11},{4,12},{5,13},{6,14},{7,15},{8,0},{9,1},... | collective-permute-start | bytes 208904 | tf_op jit(solution)/shard_map/ppermute | solution.py:41
  58.3 5.3 %collective-permute-start.13 = (f32[136,128]{1,0:T(8,128)S(1)}, f32[136,128]{1,0:T(8,128)S(1)}, u32[]{:S(2)}, u32[]{:S(2)}) collective-permute-start(f32[136,128]{1,0:T(8,128)S(1)} %get-tuple-element.50), channel_id=1, source_target_pairs={{0,4},{1,5},{2,6},{3,7},{4,8},{5,9},{6,10},{7,11},{8,12},{9,13},{1... | collective-permute-start | bytes 208904 | tf_op jit(solution)/shard_map/ppermute | solution.py:41
  58.6 6.4 %collective-permute-start.14 = (f32[136,128]{1,0:T(8,128)S(1)}, f32[136,128]{1,0:T(8,128)S(1)}, u32[]{:S(2)}, u32[]{:S(2)}) collective-permute-start(f32[136,128]{1,0:T(8,128)S(1)} %get-tuple-element.51), channel_id=1, source_target_pairs={{0,12},{1,13},{2,14},{3,15},{4,0},{5,1},{6,2},{7,3},{8,4},{9,5},{1... | collective-permute-start | bytes 208904 | tf_op jit(solution)/shard_map/ppermute | solution.py:41
  65.0 3.2 %collective-permute-start.15 = (f32[64,128]{1,0:T(8,128)S(1)}, f32[64,128]{1,0:T(8,128)S(1)}, u32[]{:S(2)}, u32[]{:S(2)}) collective-permute-start(f32[64,128]{1,0:T(8,128)S(1)} %get-tuple-element.53), channel_id=1, source_target_pairs={{0,1},{1,0},{2,3},{3,2},{4,5},{5,4},{6,7},{7,6},{8,9},{9,8},{10,11... | collective-permute-start | bytes 98312 | tf_op jit(solution)/shard_map/ppermute | solution.py:41
  68.9 4.8 %collective-permute-start.16 = (f32[16,1152]{1,0:T(8,128)S(1)}, f32[16,1152]{1,0:T(8,128)S(1)}, u32[]{:S(2)}, u32[]{:S(2)}) collective-permute-start(f32[16,1152]{1,0:T(8,128)S(1)} %shard_map.76.rest_0_), channel_id=1, source_target_pairs={{0,128},{1,129},{2,130},{3,131},{4,132},{5,133},{6,134},{7,135},{8... | collective-permute-start | bytes 221192 | tf_op jit(solution)/shard_map/ppermute | solution.py:41
  70.8 4.5 %collective-permute-start.17 = (f32[16,1152]{1,0:T(8,128)S(1)}, f32[16,1152]{1,0:T(8,128)S(1)}, u32[]{:S(2)}, u32[]{:S(2)}) collective-permute-start(f32[16,1152]{1,0:T(8,128)S(1)} %shard_map.76.rest_0_), channel_id=1, source_target_pairs={{0,64},{1,65},{2,66},{3,67},{4,68},{5,69},{6,70},{7,71},{8,72},{9,... | collective-permute-start | bytes 221192 | tf_op jit(solution)/shard_map/ppermute | solution.py:41
  72.2 3.6 %collective-permute-start.18 = (f32[16,1152]{1,0:T(8,128)S(1)}, f32[16,1152]{1,0:T(8,128)S(1)}, u32[]{:S(2)}, u32[]{:S(2)}) collective-permute-start(f32[16,1152]{1,0:T(8,128)S(1)} %shard_map.76.rest_0_), channel_id=1, source_target_pairs={{0,192},{1,193},{2,194},{3,195},{4,196},{5,197},{6,198},{7,199},{8... | collective-permute-start | bytes 221192 | tf_op jit(solution)/shard_map/ppermute | solution.py:41

commit v3 on v2

--- a/solution.py
+++ b/solution.py
@@ -70,12 +70,12 @@
     return jax.ShapeDtypeStruct(dims, dtype)
 
 
-def call(kernel, outs, spaces, args, scratch=()):
+def call(kernel, outs, spaces, args, scratch=(), places=None):
     return pl.pallas_call(
         kernel,
         out_shape=outs,
         in_specs=[pl.BlockSpec(memory_space=s) for s in spaces],
-        out_specs=jax.tree.map(lambda _: pl.BlockSpec(memory_space=VMEM), outs),
+        out_specs=places or jax.tree.map(lambda _: pl.BlockSpec(memory_space=VMEM), outs),
         scratch_shapes=list(scratch),
         compiler_params=pltpu.CompilerParams(vmem_limit_bytes=44 << 20),
     )(*args)
@@ -270,15 +270,21 @@
 
 
 def place_kernel(where, *rest):
-    ins, (fresh_ref, count_ref) = rest[:-2], rest[-2:]
-    part, width = ins[0].shape[0], fresh_ref.shape[1]
+    ins, (fresh_hbm, count_ref, fresh, sems) = rest[:-4], rest[-4:]
+    part, width = ins[0].shape[0], fresh.shape[2]
     kinds = count_ref.shape[1]
-    for step, r in zip(TURNS, ins):
+    copies = []
+    for j, (step, r) in enumerate(zip(TURNS, ins)):
         q = lax.rem(where[5] - step + N, N)
-        fresh_ref[pl.ds(pl.multiple_of(q * part, part), part), :] = r[:, :width]
+        fresh[j] = r[:, :width]
+        rows = pl.ds(pl.multiple_of(q * part, part), part)
+        copies.append(pltpu.make_async_copy(fresh.at[j], fresh_hbm.at[rows, :], sems.at[j]))
+        copies[-1].start()
         for k in range(part // kinds):
             line = r[k : k + 1, width : width + kinds]
             count_ref[pl.ds(q * (part // kinds) + k, 1), :] = line.astype(jnp.int32)
+    for copy in copies:
+        copy.wait()
 
 
 def per_device(pool_rows, sample_index, cluster_id, child_id, old_centroids):
@@ -353,6 +359,8 @@
         [shape(block * kinds, width), shape(block, kinds, dtype=jnp.int32)],
         [SMEM] + [VMEM] * N,
         [where, *quarters],
+        [VMEM((N, part, width), jnp.float32), DMA((N,))],
+        [pl.BlockSpec(memory_space=HBM), pl.BlockSpec(memory_space=VMEM)],
     )
     return centroids.reshape(block, kinds, width), counts
 

time: 77.3 us -> 78 us (level)
  no operation moved by 1% of the time
where the time goes in v3:
time: 78 us; the launch traced here: 77.9 us
  starting transfers between devices  39.4 us (51%)
  waiting for transfers between devices  22.7 us (29%)
  Pallas kernels  14 us (18%)
  between operations  0.89 us (1%)
    ppermute x19, starting transfers between devices, permute(): return lax.ppermute(value, AXES, pairs)  39.4 us
    ppermute x19, waiting for transfers between devices, permute(): return lax.ppermute(value, AXES, pairs)  22.7 us
    pallas_call x10, Pallas kernels, call(): pl.pallas_call(kernel, out_shape=outs, in_specs=[pl.BlockSpec(memory_spac...  14 us
  transfers between devices with their start and end apart: 19, of which 15 were waited for; matrix products, arithmetic and copies ran while one was open for 1% of the time, Pallas kernels for 10%

profile of v3, /device:TPU:1, one launch (start us, length us, event | category | flops | bytes accessed | tf_op | source)
XLA Modules:
  0.0 77.9 jit_solution(4164701772383887324)
XLA Ops:
  0.6 3.3 %collective-permute-start.1 = (bf16[1024,1024]{1,0:T(8,128)(2,1)}, bf16[1024,1024]{1,0:T(8,128)(2,1)S(1)}, u32[]{:S(2)}, u32[]{:S(2)}) collective-permute-start(bf16[1024,1024]{1,0:T(8,128)(2,1)} %pool_hbm.1), channel_id=1, source_target_pairs={{0,1},{1,0},{2,3},{3,2},{4,5},{5,4},{6,7},{7,6},{8,9},{9,8},{10,11... | collective-permute-start | bytes 6291464 | tf_op jit(solution)/shard_map/ppermute | solution.py:41
  3.9 0.7 pad_add_fusion
  4.7 0.1 collective-permute-start
  4.8 0.1 stack.39.where
  4.9 1.5 %shard_map.68 = (f32[256,8]{1,0:T(8,128)S(1)}, f32[16,128]{1,0:T(8,128)S(1)}) custom-call(s32[6]{0:T(128)S(1)} %stack.39.where, s32[3,1,1024]{2,1,0:T(1,128)S(1)} %reshape.14.ints_ref), custom_call_target="tpu_custom_call" | custom-call | tf_op jit(solution)/shard_map/pallas_call | solution.py:74
  6.4 1.6 %collective-permute-done.ints_ref = s32[3,1,1024]{2,1,0:T(1,128)S(1)} collective-permute-done((s32[3,1,1024]{2,1,0:T(1,128)S(1)}, s32[3,1,1024]{2,1,0:T(1,128)S(1)}, u32[]{:S(2)}, u32[]{:S(2)}) %collective-permute-start) | collective-permute-done | bytes 12320 | tf_op jit(solution)/shard_map/ppermute | solution.py:41
  7.9 2.1 %shard_map.69 = (f32[256,8]{1,0:T(8,128)S(1)}, f32[16,128]{1,0:T(8,128)S(1)}, bf16[1024,1024]{1,0:T(8,128)(2,1)S(1)}) custom-call(s32[6]{0:T(128)S(1)} %stack.39.where, s32[3,1,1024]{2,1,0:T(1,128)S(1)} %collective-permute-done.ints_ref, bf16[1024,1024]{1,0:T(8,128)(2,1)} %pool_hbm.1), custom_call_target="tpu_custom_call" | custom-call | tf_op jit(solution)/shard_map/pallas_call | solution.py:74
  10.1 0.0 collective-permute-done.1.came_pool
  10.1 2.4 %shard_map.70 = (bf16[2056,128]{1,0:T(8,128)(2,1)S(1)}, bf16[2056,128]{1,0:T(8,128)(2,1)S(1)}, bf16[2056,128]{1,0:T(8,128)(2,1)S(1)}) custom-call(s32[6]{0:T(128)S(1)} %stack.39.where, f32[256,8]{1,0:T(8,128)S(1)} %get-tuple-element.29.own_source, f32[16,128]{1,0:T(8,128)S(1)} %get-tuple-element.30.own_label, f32[256,8]{1,0:T(8,128)S(1)} %get-tuple-element.31.came_source, ...), custom_call_target="tpu_custom_call" | custom-call | tf_op jit(solution)/shard_map/pallas_call | solution.py:74
  12.5 6.6 %collective-permute-start.2 = (bf16[2056,128]{1,0:T(8,128)(2,1)S(1)}, bf16[2056,128]{1,0:T(8,128)(2,1)S(1)}, u32[]{:S(2)}, u32[]{:S(2)}) collective-permute-start(bf16[2056,128]{1,0:T(8,128)(2,1)S(1)} %get-tuple-element.34), channel_id=1, source_target_pairs={{0,34},{1,143},{2,32},{3,133},{4,38},{5,131},{6,36},{7,137},{8,42}... | collective-permute-start | bytes 1579016 | tf_op jit(solution)/shard_map/ppermute | solution.py:41
  19.1 0.1 collective-permute-start.3
  19.1 0.3 collective-permute-start.4
  19.5 3.5 %shard_map.71 = (bf16[2056,128]{1,0:T(8,128)(2,1)S(1)}, bf16[2056,128]{1,0:T(8,128)(2,1)S(1)}, bf16[2056,128]{1,0:T(8,128)(2,1)S(1)}, bf16[2056,128]{1,0:T(8,128)(2,1)S(1)}, bf16[2056,128]{1,0:T(8,128)(2,1)S(1)}) custom-call(s32[6]{0:T(128)S(1)} %stack.39.where, f32[256,8]{1,0:T(8,128)S(1)} %get-tuple-element.29.own_source, ...), custom_call_target="tpu_custom_call" | custom-call | tf_op jit(solution)/shard_map/pallas_call | solution.py:74
  22.9 3.4 %collective-permute-start.5 = (bf16[2056,128]{1,0:T(8,128)(2,1)S(1)}, bf16[2056,128]{1,0:T(8,128)(2,1)S(1)}, u32[]{:S(2)}, u32[]{:S(2)}) collective-permute-start(bf16[2056,128]{1,0:T(8,128)(2,1)S(1)} %get-tuple-element.37), channel_id=1, source_target_pairs={{0,18},{1,79},{2,16},{3,69},{4,22},{5,67},{6,20},{7,73},{8,26},{9,... | collective-permute-start | bytes 1579016 | tf_op jit(solution)/shard_map/ppermute | solution.py:41
  26.4 1.4 %collective-permute-start.6 = (bf16[2056,128]{1,0:T(8,128)(2,1)S(1)}, bf16[2056,128]{1,0:T(8,128)(2,1)S(1)}, u32[]{:S(2)}, u32[]{:S(2)}) collective-permute-start(bf16[2056,128]{1,0:T(8,128)(2,1)S(1)} %get-tuple-element.40), channel_id=1, source_target_pairs={{0,48},{1,193},{2,50},{3,195},{4,52},{5,197},{6,54},{7,199},{8,56}... | collective-permute-start | bytes 1579016 | tf_op jit(solution)/shard_map/ppermute | solution.py:41
  27.8 0.0 collective-permute-done.2.rest_0_
  27.8 2.9 %collective-permute-start.7 = (bf16[2056,128]{1,0:T(8,128)(2,1)S(1)}, bf16[2056,128]{1,0:T(8,128)(2,1)S(1)}, u32[]{:S(2)}, u32[]{:S(2)}) collective-permute-start(bf16[2056,128]{1,0:T(8,128)(2,1)S(1)} %get-tuple-element.41), channel_id=1, source_target_pairs={{0,50},{1,207},{2,48},{3,197},{4,54},{5,195},{6,52},{7,201},{8,58}... | collective-permute-start | bytes 1579016 | tf_op jit(solution)/shard_map/ppermute | solution.py:41
  30.7 0.9 %collective-permute-done.3.rest_1_ = bf16[2056,128]{1,0:T(8,128)(2,1)S(1)} collective-permute-done((bf16[2056,128]{1,0:T(8,128)(2,1)S(1)}, bf16[2056,128]{1,0:T(8,128)(2,1)S(1)}, u32[]{:S(2)}, u32[]{:S(2)}) %collective-permute-start.3) | collective-permute-done | bytes 526368 | tf_op jit(solution)/shard_map/ppermute | solution.py:41
  31.6 0.4 collective-permute-start.8
  32.0 0.0 collective-permute-done.4.rest_2_
  32.0 5.0 %collective-permute-done.5.rest_3_ = bf16[2056,128]{1,0:T(8,128)(2,1)S(1)} collective-permute-done((bf16[2056,128]{1,0:T(8,128)(2,1)S(1)}, bf16[2056,128]{1,0:T(8,128)(2,1)S(1)}, u32[]{:S(2)}, u32[]{:S(2)}) %collective-permute-start.5) | collective-permute-done | bytes 526368 | tf_op jit(solution)/shard_map/ppermute | solution.py:41
  37.0 1.0 %shard_map.72 = (f32[512,512]{1,0:T(8,128)S(1)}, f32[2,8,256]{2,1,0:T(8,128)S(1)}) custom-call(bf16[2056,128]{1,0:T(8,128)(2,1)S(1)} %collective-permute-done.2.rest_0_, bf16[2056,128]{1,0:T(8,128)(2,1)S(1)} %collective-permute-done.3.rest_1_, bf16[2056,128]{1,0:T(8,128)(2,1)S(1)} %collective-permute-done.4.rest_2_, ...), custom_call_target="tpu_custom_call" | custom-call | tf_op jit(solution)/shard_map/pallas_call | solution.py:74
  38.0 2.2 %collective-permute-done.6.rest_0_ = bf16[2056,128]{1,0:T(8,128)(2,1)S(1)} collective-permute-done((bf16[2056,128]{1,0:T(8,128)(2,1)S(1)}, bf16[2056,128]{1,0:T(8,128)(2,1)S(1)}, u32[]{:S(2)}, u32[]{:S(2)}) %collective-permute-start.6) | collective-permute-done | bytes 526368 | tf_op jit(solution)/shard_map/ppermute | solution.py:41
  40.2 2.0 %collective-permute-done.7.rest_1_ = bf16[2056,128]{1,0:T(8,128)(2,1)S(1)} collective-permute-done((bf16[2056,128]{1,0:T(8,128)(2,1)S(1)}, bf16[2056,128]{1,0:T(8,128)(2,1)S(1)}, u32[]{:S(2)}, u32[]{:S(2)}) %collective-permute-start.7) | collective-permute-done | bytes 526368 | tf_op jit(solution)/shard_map/ppermute | solution.py:41
  42.2 0.4 collective-permute-done.8.rest_2_
  42.6 0.0 copy-start
  42.6 0.9 %shard_map.73 = (f32[520,128]{1,0:T(8,128)S(1)}, f32[520,128]{1,0:T(8,128)S(1)}, f32[520,128]{1,0:T(8,128)S(1)}, f32[520,128]{1,0:T(8,128)S(1)}) custom-call(f32[512,512]{1,0:T(8,128)S(1)} %get-tuple-element.38.sum_ref, f32[2,8,256]{2,1,0:T(8,128)S(1)} %get-tuple-element.39.tally_ref, bf16[2056,128]{1,0:T(8,128)(2,1)S(1)} %collective-permute-done.6.rest_0_, ...), custom_call_target="tpu_custom_call" | custom-call | tf_op jit(solution)/shard_map/pallas_call | solution.py:74
  43.5 2.8 %collective-permute-start.9 = (f32[520,128]{1,0:T(8,128)S(1)}, f32[520,128]{1,0:T(8,128)S(1)}, u32[]{:S(2)}, u32[]{:S(2)}) collective-permute-start(f32[520,128]{1,0:T(8,128)S(1)} %get-tuple-element.45), channel_id=1, source_target_pairs={{0,128},{1,33},{2,130},{3,35},{4,132},{5,37},{6,134},{7,39},{8,136... | collective-permute-start | bytes 798728 | tf_op jit(solution)/shard_map/ppermute | solution.py:41
  46.4 0.3 collective-permute-start.10
  46.7 2.4 %collective-permute-start.11 = (f32[520,128]{1,0:T(8,128)S(1)}, f32[520,128]{1,0:T(8,128)S(1)}, u32[]{:S(2)}, u32[]{:S(2)}) collective-permute-start(f32[520,128]{1,0:T(8,128)S(1)} %get-tuple-element.47), channel_id=1, source_target_pairs={{0,192},{1,49},{2,194},{3,51},{4,196},{5,53},{6,198},{7,55},{8,200... | collective-permute-start | bytes 798728 | tf_op jit(solution)/shard_map/ppermute | solution.py:41
  49.0 1.4 %collective-permute-done.9.rest_1_ = f32[520,128]{1,0:T(8,128)S(1)} collective-permute-done((f32[520,128]{1,0:T(8,128)S(1)}, f32[520,128]{1,0:T(8,128)S(1)}, u32[]{:S(2)}, u32[]{:S(2)}) %collective-permute-start.9) | collective-permute-done | bytes 266272 | tf_op jit(solution)/shard_map/ppermute | solution.py:41
  50.4 2.8 %collective-permute-done.10.rest_2_ = f32[520,128]{1,0:T(8,128)S(1)} collective-permute-done((f32[520,128]{1,0:T(8,128)S(1)}, f32[520,128]{1,0:T(8,128)S(1)}, u32[]{:S(2)}, u32[]{:S(2)}) %collective-permute-start.10) | collective-permute-done | bytes 266272 | tf_op jit(solution)/shard_map/ppermute | solution.py:41
  53.2 0.1 collective-permute-done.11.rest_3_
  53.3 0.1 shard_map.74
  53.4 4.9 %collective-permute-start.12 = (f32[136,128]{1,0:T(8,128)S(1)}, f32[136,128]{1,0:T(8,128)S(1)}, u32[]{:S(2)}, u32[]{:S(2)}) collective-permute-start(f32[136,128]{1,0:T(8,128)S(1)} %get-tuple-element.49), channel_id=1, source_target_pairs={{0,8},{1,9},{2,10},{3,11},{4,12},{5,13},{6,14},{7,15},{8,0},{9,1},... | collective-permute-start | bytes 208904 | tf_op jit(solution)/shard_map/ppermute | solution.py:41
  58.3 0.3 collective-permute-start.13
  58.6 3.3 %collective-permute-start.14 = (f32[136,128]{1,0:T(8,128)S(1)}, f32[136,128]{1,0:T(8,128)S(1)}, u32[]{:S(2)}, u32[]{:S(2)}) collective-permute-start(f32[136,128]{1,0:T(8,128)S(1)} %get-tuple-element.51), channel_id=1, source_target_pairs={{0,12},{1,13},{2,14},{3,15},{4,0},{5,1},{6,2},{7,3},{8,4},{9,5},{1... | collective-permute-start | bytes 208904 | tf_op jit(solution)/shard_map/ppermute | solution.py:41
  61.9 0.0 collective-permute-done.12.rest_1_
  61.9 1.7 %collective-permute-done.13.rest_2_ = f32[136,128]{1,0:T(8,128)S(1)} collective-permute-done((f32[136,128]{1,0:T(8,128)S(1)}, f32[136,128]{1,0:T(8,128)S(1)}, u32[]{:S(2)}, u32[]{:S(2)}) %collective-permute-start.13) | collective-permute-done | bytes 69664 | tf_op jit(solution)/shard_map/ppermute | solution.py:41
  63.6 1.4 %collective-permute-done.14.rest_3_ = f32[136,128]{1,0:T(8,128)S(1)} collective-permute-done((f32[136,128]{1,0:T(8,128)S(1)}, f32[136,128]{1,0:T(8,128)S(1)}, u32[]{:S(2)}, u32[]{:S(2)}) %collective-permute-start.14) | collective-permute-done | bytes 69664 | tf_op jit(solution)/shard_map/ppermute | solution.py:41
  65.0 2.4 %collective-permute-start.15 = (f32[64,128]{1,0:T(8,128)S(1)}, f32[64,128]{1,0:T(8,128)S(1)}, u32[]{:S(2)}, u32[]{:S(2)}) collective-permute-start(f32[64,128]{1,0:T(8,128)S(1)} %get-tuple-element.53), channel_id=1, source_target_pairs={{0,1},{1,0},{2,3},{3,2},{4,5},{5,4},{6,7},{7,6},{8,9},{9,8},{10,11... | collective-permute-start | bytes 98312 | tf_op jit(solution)/shard_map/ppermute | solution.py:41
  67.4 0.9 %collective-permute-done.15.came_ref = f32[64,128]{1,0:T(8,128)S(1)} collective-permute-done((f32[64,128]{1,0:T(8,128)S(1)}, f32[64,128]{1,0:T(8,128)S(1)}, u32[]{:S(2)}, u32[]{:S(2)}) %collective-permute-start.15) | collective-permute-done | bytes 32800 | tf_op jit(solution)/shard_map/ppermute | solution.py:41
  68.2 0.0 copy-done
  68.3 0.6 shard_map.76.rest_0_
  68.9 1.9 %collective-permute-start.16 = (f32[16,1152]{1,0:T(8,128)S(1)}, f32[16,1152]{1,0:T(8,128)S(1)}, u32[]{:S(2)}, u32[]{:S(2)}) collective-permute-start(f32[16,1152]{1,0:T(8,128)S(1)} %shard_map.76.rest_0_), channel_id=1, source_target_pairs={{0,128},{1,129},{2,130},{3,131},{4,132},{5,133},{6,134},{7,135},{8... | collective-permute-start | bytes 221192 | tf_op jit(solution)/shard_map/ppermute | solution.py:41
  70.8 1.4 %collective-permute-start.17 = (f32[16,1152]{1,0:T(8,128)S(1)}, f32[16,1152]{1,0:T(8,128)S(1)}, u32[]{:S(2)}, u32[]{:S(2)}) collective-permute-start(f32[16,1152]{1,0:T(8,128)S(1)} %shard_map.76.rest_0_), channel_id=1, source_target_pairs={{0,64},{1,65},{2,66},{3,67},{4,68},{5,69},{6,70},{7,71},{8,72},{9,... | collective-permute-start | bytes 221192 | tf_op jit(solution)/shard_map/ppermute | solution.py:41
  72.2 1.2 %collective-permute-start.18 = (f32[16,1152]{1,0:T(8,128)S(1)}, f32[16,1152]{1,0:T(8,128)S(1)}, u32[]{:S(2)}, u32[]{:S(2)}) collective-permute-start(f32[16,1152]{1,0:T(8,128)S(1)} %shard_map.76.rest_0_), channel_id=1, source_target_pairs={{0,192},{1,193},{2,194},{3,195},{4,196},{5,197},{6,198},{7,199},{8... | collective-permute-start | bytes 221192 | tf_op jit(solution)/shard_map/ppermute | solution.py:41
  73.4 0.2 collective-permute-done.16.rest_1_
  73.7 1.6 %collective-permute-done.17.rest_2_ = f32[16,1152]{1,0:T(8,128)S(1)} collective-permute-done((f32[16,1152]{1,0:T(8,128)S(1)}, f32[16,1152]{1,0:T(8,128)S(1)}, u32[]{:S(2)}, u32[]{:S(2)}) %collective-permute-start.17) | collective-permute-done | bytes 73760 | tf_op jit(solution)/shard_map/ppermute | solution.py:41
  75.3 0.6 collective-permute-done.18.rest_3_
  75.8 1.9 %shard_map.77 = (f32[64,1024]{1,0:T(8,128)}, s32[8,8]{1,0:T(8,128)}) custom-call(s32[6]{0:T(128)S(1)} %stack.39.where, f32[16,1152]{1,0:T(8,128)S(1)} %shard_map.76.rest_0_, f32[16,1152]{1,0:T(8,128)S(1)} %collective-permute-done.16.rest_1_, f32[16,1152]{1,0:T(8,128)S(1)} %collective-permute-done.17.rest_2_, f32[16,1152]{1,0:T(8,128)S(1)} %collective-permute-done.18.rest_3_), custom_call_target="tpu_custom_call" | custom-call | tf_op jit(solution)/shard_map/pallas_call | solution.py:74
  (2 shorter events, 0.0 us)
Async XLA Ops:
  0.6 9.5 %collective-permute-start.1 = (bf16[1024,1024]{1,0:T(8,128)(2,1)}, bf16[1024,1024]{1,0:T(8,128)(2,1)S(1)}, u32[]{:S(2)}, u32[]{:S(2)}) collective-permute-start(bf16[1024,1024]{1,0:T(8,128)(2,1)} %pool_hbm.1), channel_id=1, source_target_pairs={{0,1},{1,0},{2,3},{3,2},{4,5},{5,4},{6,7},{7,6},{8,9},{9,8},{10,11... | collective-permute-start | bytes 6291464 | tf_op jit(solution)/shard_map/ppermute | solution.py:41
  4.7 3.3 %collective-permute-start = (s32[3,1,1024]{2,1,0:T(1,128)S(1)}, s32[3,1,1024]{2,1,0:T(1,128)S(1)}, u32[]{:S(2)}, u32[]{:S(2)}) collective-permute-start(s32[3,1,1024]{2,1,0:T(1,128)S(1)} %reshape.14.ints_ref), channel_id=1, source_target_pairs={{0,1},{1,0},{2,3},{3,2},{4,5},{5,4},{6,7},{7,6},{8,9},{9,8},{10,11... | collective-permute-start | bytes 36872 | tf_op jit(solution)/shard_map/ppermute | solution.py:41
  12.5 15.3 %collective-permute-start.2 = (bf16[2056,128]{1,0:T(8,128)(2,1)S(1)}, bf16[2056,128]{1,0:T(8,128)(2,1)S(1)}, u32[]{:S(2)}, u32[]{:S(2)}) collective-permute-start(bf16[2056,128]{1,0:T(8,128)(2,1)S(1)} %get-tuple-element.34), channel_id=1, source_target_pairs={{0,34},{1,143},{2,32},{3,133},{4,38},{5,131},{6,36},{7,137},{8,42}... | collective-permute-start | bytes 1579016 | tf_op jit(solution)/shard_map/ppermute | solution.py:41
  19.1 12.5 %collective-permute-start.3 = (bf16[2056,128]{1,0:T(8,128)(2,1)S(1)}, bf16[2056,128]{1,0:T(8,128)(2,1)S(1)}, u32[]{:S(2)}, u32[]{:S(2)}) collective-permute-start(bf16[2056,128]{1,0:T(8,128)(2,1)S(1)} %get-tuple-element.35), channel_id=1, source_target_pairs={{0,32},{1,129},{2,34},{3,131},{4,36},{5,133},{6,38},{7,135},{8,40}... | collective-permute-start | bytes 1579016 | tf_op jit(solution)/shard_map/ppermute | solution.py:41
  19.1 12.9 %collective-permute-start.4 = (bf16[2056,128]{1,0:T(8,128)(2,1)S(1)}, bf16[2056,128]{1,0:T(8,128)(2,1)S(1)}, u32[]{:S(2)}, u32[]{:S(2)}) collective-permute-start(bf16[2056,128]{1,0:T(8,128)(2,1)S(1)} %get-tuple-element.36), channel_id=1, source_target_pairs={{0,2},{1,15},{2,0},{3,5},{4,6},{5,3},{6,4},{7,9},{8,10},{9,7},{10,... | collective-permute-start | bytes 1579016 | tf_op jit(solution)/shard_map/ppermute | solution.py:41
  22.9 14.1 %collective-permute-start.5 = (bf16[2056,128]{1,0:T(8,128)(2,1)S(1)}, bf16[2056,128]{1,0:T(8,128)(2,1)S(1)}, u32[]{:S(2)}, u32[]{:S(2)}) collective-permute-start(bf16[2056,128]{1,0:T(8,128)(2,1)S(1)} %get-tuple-element.37), channel_id=1, source_target_pairs={{0,18},{1,79},{2,16},{3,69},{4,22},{5,67},{6,20},{7,73},{8,26},{9,... | collective-permute-start | bytes 1579016 | tf_op jit(solution)/shard_map/ppermute | solution.py:41
  26.4 13.9 %collective-permute-start.6 = (bf16[2056,128]{1,0:T(8,128)(2,1)S(1)}, bf16[2056,128]{1,0:T(8,128)(2,1)S(1)}, u32[]{:S(2)}, u32[]{:S(2)}) collective-permute-start(bf16[2056,128]{1,0:T(8,128)(2,1)S(1)} %get-tuple-element.40), channel_id=1, source_target_pairs={{0,48},{1,193},{2,50},{3,195},{4,52},{5,197},{6,54},{7,199},{8,56}... | collective-permute-start | bytes 1579016 | tf_op jit(solution)/shard_map/ppermute | solution.py:41
  27.8 14.5 %collective-permute-start.7 = (bf16[2056,128]{1,0:T(8,128)(2,1)S(1)}, bf16[2056,128]{1,0:T(8,128)(2,1)S(1)}, u32[]{:S(2)}, u32[]{:S(2)}) collective-permute-start(bf16[2056,128]{1,0:T(8,128)(2,1)S(1)} %get-tuple-element.41), channel_id=1, source_target_pairs={{0,50},{1,207},{2,48},{3,197},{4,54},{5,195},{6,52},{7,201},{8,58}... | collective-permute-start | bytes 1579016 | tf_op jit(solution)/shard_map/ppermute | solution.py:41
  31.6 11.0 %collective-permute-start.8 = (bf16[2056,128]{1,0:T(8,128)(2,1)S(1)}, bf16[2056,128]{1,0:T(8,128)(2,1)S(1)}, u32[]{:S(2)}, u32[]{:S(2)}) collective-permute-start(bf16[2056,128]{1,0:T(8,128)(2,1)S(1)} %get-tuple-element.42), channel_id=1, source_target_pairs={{0,16},{1,65},{2,18},{3,67},{4,20},{5,69},{6,22},{7,71},{8,24},{9,... | collective-permute-start | bytes 1579016 | tf_op jit(solution)/shard_map/ppermute | solution.py:41
  42.6 25.7 %copy-start = (f32[8,8,1024]{2,1,0:T(8,128)S(1)}, f32[8,8,1024]{2,1,0:T(8,128)}, u32[]{:S(2)}) copy-start(f32[8,8,1024]{2,1,0:T(8,128)} %param.9) | copy-start | bytes 786436
  43.5 6.9 %collective-permute-start.9 = (f32[520,128]{1,0:T(8,128)S(1)}, f32[520,128]{1,0:T(8,128)S(1)}, u32[]{:S(2)}, u32[]{:S(2)}) collective-permute-start(f32[520,128]{1,0:T(8,128)S(1)} %get-tuple-element.45), channel_id=1, source_target_pairs={{0,128},{1,33},{2,130},{3,35},{4,132},{5,37},{6,134},{7,39},{8,136... | collective-permute-start | bytes 798728 | tf_op jit(solution)/shard_map/ppermute | solution.py:41
  46.4 6.9 %collective-permute-start.10 = (f32[520,128]{1,0:T(8,128)S(1)}, f32[520,128]{1,0:T(8,128)S(1)}, u32[]{:S(2)}, u32[]{:S(2)}) collective-permute-start(f32[520,128]{1,0:T(8,128)S(1)} %get-tuple-element.46), channel_id=1, source_target_pairs={{0,64},{1,17},{2,66},{3,19},{4,68},{5,21},{6,70},{7,23},{8,72},{9,... | collective-permute-start | bytes 798728 | tf_op jit(solution)/shard_map/ppermute | solution.py:41
  46.7 6.7 %collective-permute-start.11 = (f32[520,128]{1,0:T(8,128)S(1)}, f32[520,128]{1,0:T(8,128)S(1)}, u32[]{:S(2)}, u32[]{:S(2)}) collective-permute-start(f32[520,128]{1,0:T(8,128)S(1)} %get-tuple-element.47), channel_id=1, source_target_pairs={{0,192},{1,49},{2,194},{3,51},{4,196},{5,53},{6,198},{7,55},{8,200... | collective-permute-start | bytes 798728 | tf_op jit(solution)/shard_map/ppermute | solution.py:41
  53.4 8.5 %collective-permute-start.12 = (f32[136,128]{1,0:T(8,128)S(1)}, f32[136,128]{1,0:T(8,128)S(1)}, u32[]{:S(2)}, u32[]{:S(2)}) collective-permute-start(f32[136,128]{1,0:T(8,128)S(1)} %get-tuple-element.49), channel_id=1, source_target_pairs={{0,8},{1,9},{2,10},{3,11},{4,12},{5,13},{6,14},{7,15},{8,0},{9,1},... | collective-permute-start | bytes 208904 | tf_op jit(solution)/shard_map/ppermute | solution.py:41
  58.3 5.3 %collective-permute-start.13 = (f32[136,128]{1,0:T(8,128)S(1)}, f32[136,128]{1,0:T(8,128)S(1)}, u32[]{:S(2)}, u32[]{:S(2)}) collective-permute-start(f32[136,128]{1,0:T(8,128)S(1)} %get-tuple-element.50), channel_id=1, source_target_pairs={{0,4},{1,5},{2,6},{3,7},{4,8},{5,9},{6,10},{7,11},{8,12},{9,13},{1... | collective-permute-start | bytes 208904 | tf_op jit(solution)/shard_map/ppermute | solution.py:41
  58.6 6.4 %collective-permute-start.14 = (f32[136,128]{1,0:T(8,128)S(1)}, f32[136,128]{1,0:T(8,128)S(1)}, u32[]{:S(2)}, u32[]{:S(2)}) collective-permute-start(f32[136,128]{1,0:T(8,128)S(1)} %get-tuple-element.51), channel_id=1, source_target_pairs={{0,12},{1,13},{2,14},{3,15},{4,0},{5,1},{6,2},{7,3},{8,4},{9,5},{1... | collective-permute-start | bytes 208904 | tf_op jit(solution)/shard_map/ppermute | solution.py:41
  65.0 3.2 %collective-permute-start.15 = (f32[64,128]{1,0:T(8,128)S(1)}, f32[64,128]{1,0:T(8,128)S(1)}, u32[]{:S(2)}, u32[]{:S(2)}) collective-permute-start(f32[64,128]{1,0:T(8,128)S(1)} %get-tuple-element.53), channel_id=1, source_target_pairs={{0,1},{1,0},{2,3},{3,2},{4,5},{5,4},{6,7},{7,6},{8,9},{9,8},{10,11... | collective-permute-start | bytes 98312 | tf_op jit(solution)/shard_map/ppermute | solution.py:41
  68.9 4.8 %collective-permute-start.16 = (f32[16,1152]{1,0:T(8,128)S(1)}, f32[16,1152]{1,0:T(8,128)S(1)}, u32[]{:S(2)}, u32[]{:S(2)}) collective-permute-start(f32[16,1152]{1,0:T(8,128)S(1)} %shard_map.76.rest_0_), channel_id=1, source_target_pairs={{0,128},{1,129},{2,130},{3,131},{4,132},{5,133},{6,134},{7,135},{8... | collective-permute-start | bytes 221192 | tf_op jit(solution)/shard_map/ppermute | solution.py:41
  70.8 4.5 %collective-permute-start.17 = (f32[16,1152]{1,0:T(8,128)S(1)}, f32[16,1152]{1,0:T(8,128)S(1)}, u32[]{:S(2)}, u32[]{:S(2)}) collective-permute-start(f32[16,1152]{1,0:T(8,128)S(1)} %shard_map.76.rest_0_), channel_id=1, source_target_pairs={{0,64},{1,65},{2,66},{3,67},{4,68},{5,69},{6,70},{7,71},{8,72},{9,... | collective-permute-start | bytes 221192 | tf_op jit(solution)/shard_map/ppermute | solution.py:41
  72.2 3.6 %collective-permute-start.18 = (f32[16,1152]{1,0:T(8,128)S(1)}, f32[16,1152]{1,0:T(8,128)S(1)}, u32[]{:S(2)}, u32[]{:S(2)}) collective-permute-start(f32[16,1152]{1,0:T(8,128)S(1)} %shard_map.76.rest_0_), channel_id=1, source_target_pairs={{0,192},{1,193},{2,194},{3,195},{4,196},{5,197},{6,198},{7,199},{8... | collective-permute-start | bytes 221192 | tf_op jit(solution)/shard_map/ppermute | solution.py:41
